TPU v7x, 16 devices: a whole 2x2x2 slice. The times are simulated.
16 devices in a mesh: grp: 4 (over z, y), data: 4 (over x, core).
Axes of the slice: x: 2, y: 2, z: 2, core: 2. Of those that a mesh axis runs over, the one named last changes fastest.
Arguments:
- hidden: bfloat16 [1024, 768], P(('grp', 'data')), parts along dimension 0
- w_qkv: bfloat16 [4, 768, 1280], replicated
- w_out: bfloat16 [4, 768, 768], replicated
- norm_attn: float32 [4, 768], replicated
- norm_ffn: float32 [4, 768], replicated
- k_cache: bfloat16 [4, 1024, 256, 2, 128], P(None, ('grp', 'data')), parts along dimension 1
- v_cache: bfloat16 [4, 1024, 256, 2, 128], P(None, ('grp', 'data')), parts along dimension 1
- seq_lens: int32 [1024], P(('grp', 'data')), parts along dimension 0
- w_gate: bfloat16 [4, 768, 2048], P('data')
- w_up: bfloat16 [4, 768, 2048], P('data')
- w_down: bfloat16 [4, 2048, 768], P('data')
Outputs:
- output: bfloat16 [1024, 768], P(('grp', 'data')), parts along dimension 0
There are 4 independent parts. A program takes and returns all parts, laid end to end along the dimension named above; an argument that names none is the same for every part.
All inputs are finite; a program needn't handle non-finite values.
Results may differ from a plain program's by a relative error of at most 0.02.
Values are sent between devices in bfloat16 or wider.
A program may use at most 1 GiB of HBM per device.

v0:
```python
import jax
import jax.numpy as jnp
from jax import lax
from jax.sharding import PartitionSpec as P

NORM_EPS = 1e-5


def rms_norm(tok_rows, gain_vec):
    row_vals = tok_rows.astype(jnp.float32)
    inv_rms = lax.rsqrt(jnp.mean(row_vals * row_vals, axis=-1, keepdims=True) + NORM_EPS)
    return (row_vals * inv_rms * gain_vec).astype(jnp.bfloat16)


def attention_block(tok_rows, gain_vec, layer_qkv, layer_out, layer_keys, layer_vals, seq_lens):
    row_count = tok_rows.shape[0]
    cache_len = layer_keys.shape[1]
    kv_heads = layer_keys.shape[2]
    head_dim = layer_keys.shape[3]
    q_width = layer_out.shape[0]
    group_size = q_width // (head_dim * kv_heads)
    kv_width = kv_heads * head_dim
    score_scale = head_dim ** -0.5
    normed = rms_norm(tok_rows, gain_vec)
    qkv_rows = jnp.dot(normed, layer_qkv, preferred_element_type=jnp.float32).astype(jnp.bfloat16)
    q_heads = qkv_rows[:, :q_width].reshape(row_count, kv_heads, group_size, head_dim)
    k_new = qkv_rows[:, q_width:q_width + kv_width].reshape(row_count, kv_heads, head_dim)
    v_new = qkv_rows[:, q_width + kv_width:].reshape(row_count, kv_heads, head_dim)
    s_cache = jnp.einsum('bkgd,bskd->bkgs', q_heads, layer_keys, preferred_element_type=jnp.float32) * score_scale
    s_self = jnp.einsum('clhe,cle->clh', q_heads, k_new, preferred_element_type=jnp.float32) * score_scale
    positions = lax.broadcasted_iota(jnp.int32, (1, 1, 1, cache_len), 3)
    s_cache = jnp.where(positions < seq_lens[:, None, None, None], s_cache, -1e30)
    row_max = jnp.maximum(jnp.max(s_cache, axis=-1), s_self)
    e_cache = jnp.exp(s_cache - row_max[..., None])
    e_self = jnp.exp(s_self - row_max)
    denom_sum = jnp.sum(e_cache, axis=-1) + e_self
    p_cache = (e_cache / denom_sum[..., None]).astype(jnp.bfloat16)
    p_self = (e_self / denom_sum).astype(jnp.bfloat16)
    mixed_out = jnp.einsum('bkgs,bskd->bkgd', p_cache, layer_vals, preferred_element_type=jnp.float32)
    mixed_out = mixed_out + p_self.astype(jnp.float32)[..., None] * v_new.astype(jnp.float32)[:, :, None, :]
    attn_rows = mixed_out.astype(jnp.bfloat16).reshape(row_count, q_width)
    attn_proj = jnp.dot(attn_rows, layer_out, preferred_element_type=jnp.float32)
    return (tok_rows.astype(jnp.float32) + attn_proj).astype(jnp.bfloat16)


def partial_ffn(normed, layer_gate, layer_up, layer_down):
    gate_val = jnp.dot(normed, layer_gate, preferred_element_type=jnp.float32)
    up_val = jnp.dot(normed, layer_up, preferred_element_type=jnp.float32)
    act_rows = (jax.nn.silu(gate_val) * up_val).astype(jnp.bfloat16)
    return jnp.dot(act_rows, layer_down, preferred_element_type=jnp.float32)


def solution(mesh):
    row_spec = P(('grp', 'data'), None)
    rep_spec = P()
    cache_spec = P(None, ('grp', 'data'))
    len_spec = P(('grp', 'data'))
    owned_spec = P('data')

    def per_device(hidden, w_qkv, w_out, norm_attn, norm_ffn, k_cache, v_cache, seq_lens, w_gate, w_up, w_down):
        gate_cols = lax.all_to_all(w_gate, 'data', 2, 0, tiled=True)
        up_cols = lax.all_to_all(w_up, 'data', 2, 0, tiled=True)
        down_rows = lax.all_to_all(w_down, 'data', 1, 0, tiled=True)

        def layer_step(tok_rows, layer_args):
            layer_qkv, layer_out, gain_attn, gain_ffn, layer_keys, layer_vals, layer_gate, layer_up, layer_down = layer_args
            mid_rows = attention_block(tok_rows, gain_attn, layer_qkv, layer_out, layer_keys, layer_vals, seq_lens)
            normed = rms_norm(mid_rows, gain_ffn)
            all_normed = lax.all_gather(normed, 'data', axis=0, tiled=True)
            partial_out = partial_ffn(all_normed, layer_gate, layer_up, layer_down)
            down_val = lax.psum_scatter(partial_out, 'data', scatter_dimension=0, tiled=True)
            return (mid_rows.astype(jnp.float32) + down_val).astype(jnp.bfloat16), None

        return lax.scan(layer_step, hidden, (w_qkv, w_out, norm_attn, norm_ffn, k_cache, v_cache, gate_cols, up_cols, down_rows))[0]

    return jax.shard_map(per_device, mesh=mesh, in_specs=(row_spec, rep_spec, rep_spec, rep_spec, rep_spec, cache_spec, cache_spec, len_spec, owned_spec, owned_spec, owned_spec), out_specs=row_spec, check_vma=False)
```

profile of v0, /device:TPU:0, one launch (start us, length us, event | category | flops | bytes accessed | tf_op | source)
XLA Modules:
  0.0 461.5 jit_solution(14033393885788317889)
XLA Ops:
  6.5 15.7 %copy.50 = bf16[1,768,2048]{1,0,2:T(2,128)(2,1)} copy(bf16[1,768,2048]{2,1,0:T(8,128)(2,1)} %param.22) | data formatting | bytes 6291456 | tf_op args[9]
  22.8 31.6 %reduce.5 = bf16[2048,768]{1,0:T(8,128)(2,1)S(1)} reduce(bf16[2048,1,768]{2,1,0:T(2,128)(2,1)} %bitcast.113, bf16[]{:T(256)} %broadcast.71), dimensions={1}, to_apply=%bitcast.67.reduce_sub_computation | reduce | bytes 6291458
  54.4 2.5 reshape.69
  56.9 4.5 all-to-all-start.1
  61.4 6.9 %copy.80 = bf16[1,2048,768]{2,0,1:T(2,128)(2,1)} copy(bf16[1,2048,768]{2,1,0:T(8,128)(2,1)} %param.23) | data formatting | bytes 6291456 | tf_op args[10]
  68.2 33.3 %reduce.6 = bf16[2048,768]{1,0:T(8,128)(2,1)} reduce(bf16[2048,1,768]{2,1,0:T(2,128)(2,1)} %bitcast.118, bf16[]{:T(256)} %broadcast.71), dimensions={1}, to_apply=%bitcast.82.reduce_sub_computation | reduce | bytes 6291458
  101.5 4.5 reshape.71
  106.0 4.6 %all-to-all-start.2 = ((bf16[4,2,196608]{2,1,0:T(2,128)(2,1)}), bf16[4,2,196608]{2,1,0:T(2,128)(2,1)}, u32[]{:S(2)}, u32[]{:S(2)}) async-start(bf16[4,2,196608]{2,1,0:T(2,128)(2,1)} %reshape.71), calls=%async_computation.3 | async-start | bytes 6291456 | tf_op jit(solution)/shard_map/all_to_all | solution.py:63
  110.7 15.8 %copy.49 = bf16[1,768,2048]{1,0,2:T(2,128)(2,1)} copy(bf16[1,768,2048]{2,1,0:T(8,128)(2,1)} %param.21) | data formatting | bytes 6291456 | tf_op args[8]
  126.4 33.2 %reduce.4 = bf16[2048,768]{1,0:T(8,128)(2,1)} reduce(bf16[2048,1,768]{2,1,0:T(2,128)(2,1)} %bitcast.114, bf16[]{:T(256)} %broadcast.71), dimensions={1}, to_apply=%bitcast.65.reduce_sub_computation | reduce | bytes 6291458
  159.7 4.6 reshape.67
  164.2 4.8 %all-to-all-start = ((bf16[4,2,196608]{2,1,0:T(2,128)(2,1)}), bf16[4,2,196608]{2,1,0:T(2,128)(2,1)}, u32[]{:S(2)}, u32[]{:S(2)}) async-start(bf16[4,2,196608]{2,1,0:T(2,128)(2,1)} %reshape.67), calls=%async_computation.1 | async-start | bytes 6291456 | tf_op jit(solution)/shard_map/all_to_all | solution.py:61
  169.1 4.4 reshape.70
  173.5 5.0 %copy.63 = bf16[1,768,2048]{1,2,0:T(8,128)(2,1)} copy(bf16[1,768,2048]{1,0,2:T(2,128)(2,1)} %bitcast.115) | data formatting | bytes 6291456
  178.4 6.2 %reshape.72 = bf16[2048,1,768]{2,1,0:T(2,128)(2,1)} reshape(bf16[4,2,196608]{2,1,0:T(2,128)(2,1)} %all-to-all-done.2) | data formatting | bytes 6291456
  184.6 5.0 %copy.64 = bf16[1,2048,768]{2,1,0:T(8,128)(2,1)} copy(bf16[1,2048,768]{2,0,1:T(2,128)(2,1)} %bitcast.116) | data formatting | bytes 6291456
  189.6 16.3 %all-to-all-done = bf16[4,2,196608]{2,1,0:T(2,128)(2,1)} async-done(((bf16[4,2,196608]{2,1,0:T(2,128)(2,1)}), bf16[4,2,196608]{2,1,0:T(2,128)(2,1)}, u32[]{:S(2)}, u32[]{:S(2)}) %all-to-all-start) | async-done | bytes 3145760 | tf_op jit(solution)/shard_map/all_to_all | solution.py:61
  205.9 6.2 %reshape.68 = bf16[2048,1,768]{2,1,0:T(2,128)(2,1)} reshape(bf16[4,2,196608]{2,1,0:T(2,128)(2,1)} %all-to-all-done) | data formatting | bytes 6291456
  212.1 5.0 %copy.62 = bf16[1,768,2048]{1,2,0:T(8,128)(2,1)} copy(bf16[1,768,2048]{1,0,2:T(2,128)(2,1)} %bitcast.117) | data formatting | bytes 6291456
  217.1 237.2 %while.10 = (s32[]{:T(128)}, bf16[64,768]{1,0:T(8,128)(2,1)S(1)}, s32[64]{0:T(128)S(1)}, f32[4,768]{1,0:T(4,128)}, bf16[4,768,1280]{2,1,0:T(8,128)(2,1)}, /*inde...) while((s32[]{:T(128)}, bf16[64,768]{1,0:T(8,128)(2,1)S(1)}, ...), condition=%wide.region_6.7_spmd, body=%wide.region_0.6_spmd.sunk | while | flops 858458880 | bytes 66059692 | solution.py:74
  217.3 0.8 dynamic-slice_reduce_fusion.3
  218.0 2.1 convolution_convert_fusion.2
  220.7 14.0 %constant_dynamic-slice_fusion.3 = (bf16[1,64,256,2,128]{4,3,2,1,0:T(2,128)(2,1)}, bf16[1,64,256,2,128]{4,3,2,1,0:T(2,128)(2,1)S(1)}) fusion(bf16[4,64,256,2,128]{4,3,2,1,0:T(2,128)(2,1)} %get-tuple-element.305, s32[]{:T(128)} %get-tuple-element.286, bf16[4,64,256,2,128]{4,3,2,1,0:T(2,128)(2,1)} %get-tuple-element.304), kind=kLoop, calls=%fused_computation.58.clone.1 | loop fusion | bytes 33554436 | tf_op jit(solution)/shard_map/while/body/jit(dynamic_index_in_dim)/dynamic_slice | solution.py:74
  234.6 2.4 fusion.95
  238.1 4.6 %fusion.100 = bf16[64,2,3,128]{3,2,1,0:T(4,128)(2,1)S(1)} fusion(bf16[1,64,256,2,128]{4,3,2,1,0:T(2,128)(2,1)} %get-tuple-element.261, f32[64,2,3,256]{3,2,1,0:T(4,128)S(1)} %get-tuple-element.264, f32[64,2,3]{2,1,0:T(2,128)S(1)} %copy.95, f32[64,2,3]{2,1,0:T(2,128)S(1)} %copy.93, f32[64,2,128]{2,1,0:T(2,128)S(1)} %reshape.79, f32[64,2,3]{2,1,0:T(2,128)S(1)} %copy.96), kind=kOutput, calls=%fused_computation.16.clone.1 | convolution fusion | flops 25608192 | bytes 8950272 | tf_op jit(solution)/shard_map/while/body/eval_jaxpr/bkgs,bskd->bkgd/dot_general | solution.py:39
  242.9 1.7 multiply_reduce_fusion.2
  244.7 6.1 %all_gather.4 = bf16[256,768]{1,0:T(8,128)(2,1)S(1)} all-gather(bf16[64,768]{1,0:T(8,128)(2,1)S(1)} %multiply_convert_fusion.2), channel_id=1, replica_groups=mesh['grp'=4,'data'=4] {'data'}, dimensions={0}, use_global_device_ids=true | all-gather | bytes 491520 | tf_op jit(solution)/shard_map/while/body/eval_jaxpr/all_gather | solution.py:69
  250.9 1.5 fusion.101
  252.4 3.0 fusion.102
  255.4 20.8 %reduce-scatter.2.cloned.1.call-done = f32[64,768]{1,0:T(8,128)} async-done(((f32[256,768]{1,0:T(8,128)}), f32[64,768]{1,0:T(8,128)}) %reduce-scatter.2.cloned.1.call-update) | async-done | bytes 196624 | tf_op jit(solution)/shard_map/while/body/eval_jaxpr/reduce_scatter | solution.py:71
  276.2 0.9 add_convert_fusion.2
  277.3 0.8 dynamic-slice_reduce_fusion.3
  278.1 2.1 convolution_convert_fusion.2
  280.7 14.0 %constant_dynamic-slice_fusion.3 = (bf16[1,64,256,2,128]{4,3,2,1,0:T(2,128)(2,1)}, bf16[1,64,256,2,128]{4,3,2,1,0:T(2,128)(2,1)S(1)}) fusion(bf16[4,64,256,2,128]{4,3,2,1,0:T(2,128)(2,1)} %get-tuple-element.305, s32[]{:T(128)} %get-tuple-element.286, bf16[4,64,256,2,128]{4,3,2,1,0:T(2,128)(2,1)} %get-tuple-element.304), kind=kLoop, calls=%fused_computation.58.clone.1 | loop fusion | bytes 33554436 | tf_op jit(solution)/shard_map/while/body/jit(dynamic_index_in_dim)/dynamic_slice | solution.py:74
  294.7 2.4 fusion.95
  298.1 4.6 %fusion.100 = bf16[64,2,3,128]{3,2,1,0:T(4,128)(2,1)S(1)} fusion(bf16[1,64,256,2,128]{4,3,2,1,0:T(2,128)(2,1)} %get-tuple-element.261, f32[64,2,3,256]{3,2,1,0:T(4,128)S(1)} %get-tuple-element.264, f32[64,2,3]{2,1,0:T(2,128)S(1)} %copy.95, f32[64,2,3]{2,1,0:T(2,128)S(1)} %copy.93, f32[64,2,128]{2,1,0:T(2,128)S(1)} %reshape.79, f32[64,2,3]{2,1,0:T(2,128)S(1)} %copy.96), kind=kOutput, calls=%fused_computation.16.clone.1 | convolution fusion | flops 25608192 | bytes 8950272 | tf_op jit(solution)/shard_map/while/body/eval_jaxpr/bkgs,bskd->bkgd/dot_general | solution.py:39
  302.9 1.7 multiply_reduce_fusion.2
  304.7 6.1 %all_gather.4 = bf16[256,768]{1,0:T(8,128)(2,1)S(1)} all-gather(bf16[64,768]{1,0:T(8,128)(2,1)S(1)} %multiply_convert_fusion.2), channel_id=1, replica_groups=mesh['grp'=4,'data'=4] {'data'}, dimensions={0}, use_global_device_ids=true | all-gather | bytes 491520 | tf_op jit(solution)/shard_map/while/body/eval_jaxpr/all_gather | solution.py:69
  310.9 1.5 fusion.101
  312.4 3.0 fusion.102
  315.4 19.8 %reduce-scatter.2.cloned.1.call-done = f32[64,768]{1,0:T(8,128)} async-done(((f32[256,768]{1,0:T(8,128)}), f32[64,768]{1,0:T(8,128)}) %reduce-scatter.2.cloned.1.call-update) | async-done | bytes 196624 | tf_op jit(solution)/shard_map/while/body/eval_jaxpr/reduce_scatter | solution.py:71
  335.2 0.9 add_convert_fusion.2
  336.4 0.8 dynamic-slice_reduce_fusion.3
  337.1 2.1 convolution_convert_fusion.2
  339.8 14.0 %constant_dynamic-slice_fusion.3 = (bf16[1,64,256,2,128]{4,3,2,1,0:T(2,128)(2,1)}, bf16[1,64,256,2,128]{4,3,2,1,0:T(2,128)(2,1)S(1)}) fusion(bf16[4,64,256,2,128]{4,3,2,1,0:T(2,128)(2,1)} %get-tuple-element.305, s32[]{:T(128)} %get-tuple-element.286, bf16[4,64,256,2,128]{4,3,2,1,0:T(2,128)(2,1)} %get-tuple-element.304), kind=kLoop, calls=%fused_computation.58.clone.1 | loop fusion | bytes 33554436 | tf_op jit(solution)/shard_map/while/body/jit(dynamic_index_in_dim)/dynamic_slice | solution.py:74
  353.7 2.4 fusion.95
  357.2 4.6 %fusion.100 = bf16[64,2,3,128]{3,2,1,0:T(4,128)(2,1)S(1)} fusion(bf16[1,64,256,2,128]{4,3,2,1,0:T(2,128)(2,1)} %get-tuple-element.261, f32[64,2,3,256]{3,2,1,0:T(4,128)S(1)} %get-tuple-element.264, f32[64,2,3]{2,1,0:T(2,128)S(1)} %copy.95, f32[64,2,3]{2,1,0:T(2,128)S(1)} %copy.93, f32[64,2,128]{2,1,0:T(2,128)S(1)} %reshape.79, f32[64,2,3]{2,1,0:T(2,128)S(1)} %copy.96), kind=kOutput, calls=%fused_computation.16.clone.1 | convolution fusion | flops 25608192 | bytes 8950272 | tf_op jit(solution)/shard_map/while/body/eval_jaxpr/bkgs,bskd->bkgd/dot_general | solution.py:39
  362.0 1.7 multiply_reduce_fusion.2
  363.8 6.1 %all_gather.4 = bf16[256,768]{1,0:T(8,128)(2,1)S(1)} all-gather(bf16[64,768]{1,0:T(8,128)(2,1)S(1)} %multiply_convert_fusion.2), channel_id=1, replica_groups=mesh['grp'=4,'data'=4] {'data'}, dimensions={0}, use_global_device_ids=true | all-gather | bytes 491520 | tf_op jit(solution)/shard_map/while/body/eval_jaxpr/all_gather | solution.py:69
  369.9 1.5 fusion.101
  371.5 3.0 fusion.102
  374.5 19.8 %reduce-scatter.2.cloned.1.call-done = f32[64,768]{1,0:T(8,128)} async-done(((f32[256,768]{1,0:T(8,128)}), f32[64,768]{1,0:T(8,128)}) %reduce-scatter.2.cloned.1.call-update) | async-done | bytes 196624 | tf_op jit(solution)/shard_map/while/body/eval_jaxpr/reduce_scatter | solution.py:71
  394.3 0.9 add_convert_fusion.2
  395.5 0.8 dynamic-slice_reduce_fusion.3
  396.2 2.1 convolution_convert_fusion.2
  398.8 14.0 %constant_dynamic-slice_fusion.3 = (bf16[1,64,256,2,128]{4,3,2,1,0:T(2,128)(2,1)}, bf16[1,64,256,2,128]{4,3,2,1,0:T(2,128)(2,1)S(1)}) fusion(bf16[4,64,256,2,128]{4,3,2,1,0:T(2,128)(2,1)} %get-tuple-element.305, s32[]{:T(128)} %get-tuple-element.286, bf16[4,64,256,2,128]{4,3,2,1,0:T(2,128)(2,1)} %get-tuple-element.304), kind=kLoop, calls=%fused_computation.58.clone.1 | loop fusion | bytes 33554436 | tf_op jit(solution)/shard_map/while/body/jit(dynamic_index_in_dim)/dynamic_slice | solution.py:74
  412.8 2.4 fusion.95
  416.3 4.6 %fusion.100 = bf16[64,2,3,128]{3,2,1,0:T(4,128)(2,1)S(1)} fusion(bf16[1,64,256,2,128]{4,3,2,1,0:T(2,128)(2,1)} %get-tuple-element.261, f32[64,2,3,256]{3,2,1,0:T(4,128)S(1)} %get-tuple-element.264, f32[64,2,3]{2,1,0:T(2,128)S(1)} %copy.95, f32[64,2,3]{2,1,0:T(2,128)S(1)} %copy.93, f32[64,2,128]{2,1,0:T(2,128)S(1)} %reshape.79, f32[64,2,3]{2,1,0:T(2,128)S(1)} %copy.96), kind=kOutput, calls=%fused_computation.16.clone.1 | convolution fusion | flops 25608192 | bytes 8950272 | tf_op jit(solution)/shard_map/while/body/eval_jaxpr/bkgs,bskd->bkgd/dot_general | solution.py:39
  421.0 1.7 multiply_reduce_fusion.2
  422.9 6.1 %all_gather.4 = bf16[256,768]{1,0:T(8,128)(2,1)S(1)} all-gather(bf16[64,768]{1,0:T(8,128)(2,1)S(1)} %multiply_convert_fusion.2), channel_id=1, replica_groups=mesh['grp'=4,'data'=4] {'data'}, dimensions={0}, use_global_device_ids=true | all-gather | bytes 491520 | tf_op jit(solution)/shard_map/while/body/eval_jaxpr/all_gather | solution.py:69
  429.0 1.5 fusion.101
  430.6 3.0 fusion.102
  433.6 19.8 %reduce-scatter.2.cloned.1.call-done = f32[64,768]{1,0:T(8,128)} async-done(((f32[256,768]{1,0:T(8,128)}), f32[64,768]{1,0:T(8,128)}) %reduce-scatter.2.cloned.1.call-update) | async-done | bytes 196624 | tf_op jit(solution)/shard_map/while/body/eval_jaxpr/reduce_scatter | solution.py:71
  453.4 0.9 add_convert_fusion.2
  (101 shorter events, 8.9 us)
Async XLA Ops:
  56.9 49.1 %all-to-all-start.1 = ((bf16[4,2,196608]{2,1,0:T(2,128)(2,1)}), bf16[4,2,196608]{2,1,0:T(2,128)(2,1)S(1)}, u32[]{:S(2)}, u32[]{:S(2)}) async-start(bf16[4,2,196608]{2,1,0:T(2,128)(2,1)} %reshape.69), calls=%async_computation.2 | async-start | bytes 6291456 | tf_op jit(solution)/shard_map/all_to_all | solution.py:62
  106.0 58.2 %all-to-all-start.2 = ((bf16[4,2,196608]{2,1,0:T(2,128)(2,1)}), bf16[4,2,196608]{2,1,0:T(2,128)(2,1)}, u32[]{:S(2)}, u32[]{:S(2)}) async-start(bf16[4,2,196608]{2,1,0:T(2,128)(2,1)} %reshape.71), calls=%async_computation.3 | async-start | bytes 6291456 | tf_op jit(solution)/shard_map/all_to_all | solution.py:63
  164.2 41.7 %all-to-all-start = ((bf16[4,2,196608]{2,1,0:T(2,128)(2,1)}), bf16[4,2,196608]{2,1,0:T(2,128)(2,1)}, u32[]{:S(2)}, u32[]{:S(2)}) async-start(bf16[4,2,196608]{2,1,0:T(2,128)(2,1)} %reshape.67), calls=%async_computation.1 | async-start | bytes 6291456 | tf_op jit(solution)/shard_map/all_to_all | solution.py:61
  212.1 5.0 %copy-start.1 = (bf16[64,768]{1,0:T(8,128)(2,1)S(1)}, bf16[64,768]{1,0:T(8,128)(2,1)}, u32[]{:S(2)}) copy-start(bf16[64,768]{1,0:T(8,128)(2,1)} %param.13) | copy-start | bytes 294916
  212.1 5.0 %copy-start.2 = (s32[64]{0:T(128)S(1)}, s32[64]{0:T(128)}, u32[]{:S(2)}) copy-start(s32[64]{0:T(128)} %param.20) | copy-start | bytes 772
  217.1 59.0 %reduce-scatter.2.cloned.1.call-start = ((), (), s32[]{:S(2)}) async-start(), calls=%async_computation.4 | async-start | bytes 983040 | tf_op jit(solution)/shard_map/while/body/eval_jaxpr/reduce_scatter | solution.py:71
  277.1 58.1 %reduce-scatter.2.cloned.1.call-start = ((), (), s32[]{:S(2)}) async-start(), calls=%async_computation.4 | async-start | bytes 983040 | tf_op jit(solution)/shard_map/while/body/eval_jaxpr/reduce_scatter | solution.py:71
  336.2 58.1 %reduce-scatter.2.cloned.1.call-start = ((), (), s32[]{:S(2)}) async-start(), calls=%async_computation.4 | async-start | bytes 983040 | tf_op jit(solution)/shard_map/while/body/eval_jaxpr/reduce_scatter | solution.py:71
  395.3 58.1 %reduce-scatter.2.cloned.1.call-start = ((), (), s32[]{:S(2)}) async-start(), calls=%async_computation.4 | async-start | bytes 983040 | tf_op jit(solution)/shard_map/while/body/eval_jaxpr/reduce_scatter | solution.py:71
  454.3 0.6 copy-start
Sparse Core Ops, SparseCore 0:
  255.5 20.5 reduce-scatter.1
  315.5 19.6 reduce-scatter.1
  374.6 19.6 reduce-scatter.1
  433.7 19.6 reduce-scatter.1
where the time goes:
time: 464 us; the launch traced here: 462 us
  local copies, waits for them, and re-layouts  145 us (31%)
  other arithmetic  105 us (23%)
  waiting for transfers between devices  96.5 us (21%)
  matrix products  62.4 us (13%)
  blocking collectives  24.6 us (5%)
  starting transfers between devices  14.1 us (3%)
  between operations  13.1 us (3%)
    unnamed x3, other arithmetic  98.2 us
    unnamed x19, local copies, waits for them, and re-layouts  82.8 us
    reduce_scatter x4, waiting for transfers between devices, layer_step(): lax.psum_scatter(partial_out, 'data', scatter_dimension=0, tiled=True)  80.2 us
    dynamic_slice x8, local copies, waits for them, and re-layouts, per_device(): lax.scan(layer_step, hidden, (w_qkv, w_out, norm_attn, norm_ffn, k_cache,...  58.9 us
    all_gather x4, blocking collectives, layer_step(): all_normed = lax.all_gather(normed, 'data', axis=0, tiled=True)  24.6 us
    dot_general x4, matrix products, attention_block(): jnp.einsum('bkgs,bskd->bkgd', p_cache, layer_vals, preferred_element_type...  18.6 us
    all_to_all x1, waiting for transfers between devices, per_device(): gate_cols = lax.all_to_all(w_gate, 'data', 2, 0, tiled=True)  16.3 us
    dot_general x4, matrix products, partial_ffn(): return jnp.dot(act_rows, layer_down, preferred_element_type=jnp.float32)  12 us
  transfers between devices with their start and end apart: 7, of which 5 were waited for; matrix products, arithmetic and copies ran while one was open for 26% of the time, Pallas kernels for 0%

commit v1 on v0

v1 whole, which is shorter than its diff:
```python
import jax
import jax.numpy as jnp
from jax import lax
from jax.experimental import pallas as pl
from jax.experimental.pallas import tpu as pltpu
from jax.sharding import PartitionSpec as P

NORM_EPS = 1e-5
F32 = jnp.float32
BF16 = jnp.bfloat16
LAYERS = 4
ROWS = 64
D = 768
HD = 128
HEADS = 6
CACHE = 256
QKV = 1280
FFN = 2048
CHUNK = 16
CHUNKS = ROWS // CHUNK
SLOTS = 7
FBLK = 512
NT = (((1,), (1,)), ((), ()))


def rms(rows_bf16, gain):
    vals = rows_bf16.astype(F32)
    inv = lax.rsqrt(jnp.mean(vals * vals, axis=-1, keepdims=True) + NORM_EPS)
    return (vals * inv * gain).astype(BF16)


def kernel(hid, ga, gf, lens, wqkv, wout, kc, vc, wg, wu, wd, out,
           kbuf, vbuf, qkvw, outw, fg, fu, fd, q3, k3, v3, o3, len3, xbuf, hbuf, hg, xg, zbuf,
           ksem, vsem, wsem, fsem, hs_sem, hr_sem, xs_sem, xr_sem):
    me = lax.axis_index("data")

    def kcopy(c):
        layer, part, slot = c // CHUNKS, c % CHUNKS, c % SLOTS
        src = pl.ds(pl.multiple_of(part * CHUNK, CHUNK), CHUNK)
        return (pltpu.make_async_copy(kc.at[layer, src], kbuf.at[slot], ksem.at[slot]),
                pltpu.make_async_copy(vc.at[layer, src], vbuf.at[slot], vsem.at[slot]))

    def wcopy(layer):
        slot = layer % 2
        return (pltpu.make_async_copy(wqkv.at[layer], qkvw.at[slot], wsem.at[slot, 0]),
                pltpu.make_async_copy(wout.at[layer], outw.at[slot], wsem.at[slot, 1]))

    def fcopy():
        return (pltpu.make_async_copy(wg.at[0], fg, fsem.at[0]),
                pltpu.make_async_copy(wu.at[0], fu, fsem.at[1]),
                pltpu.make_async_copy(wd.at[0], fd, fsem.at[2]))

    def send_h(layer):
        return pltpu.make_async_remote_copy(
            src_ref=hbuf.at[layer], dst_ref=hg.at[me], send_sem=hs_sem.at[layer], recv_sem=hr_sem.at[me],
            device_id={"data": layer}, device_id_type=pl.DeviceIdType.MESH)

    def recv_h(src):
        return pltpu.make_async_remote_copy(
            src_ref=hbuf.at[0], dst_ref=hg.at[src], send_sem=hs_sem.at[0], recv_sem=hr_sem.at[src],
            device_id={"data": src}, device_id_type=pl.DeviceIdType.MESH)

    def send_x(layer, dst):
        return pltpu.make_async_remote_copy(
            src_ref=xg.at[dst], dst_ref=xbuf.at[layer + 1], send_sem=xs_sem.at[dst], recv_sem=xr_sem.at[layer],
            device_id={"data": dst}, device_id_type=pl.DeviceIdType.MESH)

    wcopy(0)[0].start()
    for c in range(CHUNKS):
        for cp in kcopy(c):
            cp.start()
    wcopy(0)[1].start()
    for cp in fcopy():
        cp.start()
    for c in range(CHUNKS, SLOTS):
        for cp in kcopy(c):
            cp.start()

    barrier = pltpu.get_barrier_semaphore()
    for step in range(1, 4):
        pl.semaphore_signal(barrier, inc=1, device_id={"data": (me + step) % 4}, device_id_type=pl.DeviceIdType.MESH)
    pl.semaphore_wait(barrier, 3)

    pick = (lax.broadcasted_iota(jnp.int32, (ROWS * 8, ROWS), 0) // 8 == lax.broadcasted_iota(jnp.int32, (ROWS * 8, ROWS), 1))
    lrow = jnp.broadcast_to(lens[...].astype(F32), (HD, ROWS)).astype(BF16)
    len3[...] = 2.0 * lax.dot_general(pick.astype(F32).astype(BF16), lrow, NT, preferred_element_type=F32)
    zrow = jnp.zeros((ROWS, HD), F32)
    for j in (6, 7):
        for ref in (q3, k3, v3):
            ref[pl.ds(j, ROWS, stride=8), :] = zrow
    xbuf[0] = hid[...]

    def layer_step(layer, carry):
        wslot = layer % 2
        wcopy(layer)[0].wait()
        normed = rms(xbuf[layer], ga[pl.ds(layer, 1), :])
        qkv = jnp.dot(normed, qkvw[wslot], preferred_element_type=F32).astype(BF16).astype(F32)
        for j in range(HEADS):
            dst = pl.ds(j, ROWS, stride=8)
            kv = j * 2 // HEADS
            q3[dst, :] = qkv[:, j * HD:(j + 1) * HD]
            k3[dst, :] = qkv[:, (HEADS + kv) * HD:(HEADS + kv + 1) * HD]
            v3[dst, :] = qkv[:, (HEADS + 2 + kv) * HD:(HEADS + 3 + kv) * HD]

        def chunk_step(part, carry):
            c = layer * CHUNKS + part
            slot = c % SLOTS
            base = pl.multiple_of(part * (CHUNK * 8), CHUNK * 8)
            rows = pl.ds(base, CHUNK * 8)
            qc = q3[rows, :]
            s_self = jnp.sum(qc * k3[rows, :], axis=-1, keepdims=True) * (HD ** -0.5)
            kcopy(c)[0].wait()
            zero = jnp.zeros((8, HD), F32)
            scores = []
            for i in range(CHUNK // 2):
                qa = qc[16 * i:16 * i + 8]
                qb = qc[16 * i + 8:16 * i + 16]
                lhs = jnp.concatenate([jnp.concatenate([qa, zero], 1), jnp.concatenate([zero, qb], 1)], 0).astype(BF16)
                keys = jnp.concatenate([kbuf[slot, 2 * i], kbuf[slot, 2 * i + 1]], 1)
                scores.append(lax.dot_general(lhs, keys, NT, preferred_element_type=F32))
            s = jnp.concatenate(scores, 0) * (HD ** -0.5)
            col = lax.broadcasted_iota(jnp.int32, s.shape, 1)
            head = lax.broadcasted_iota(jnp.int32, s.shape, 0) % 8
            lim = len3[rows, :]
            lim = jnp.concatenate([lim] * (2 * CACHE // HD), 1)
            good = (col % 2 == head // 3) & (col.astype(F32) < lim)
            s = jnp.where(good, s, -1e30)
            top = jnp.maximum(jnp.max(s, axis=-1, keepdims=True), s_self)
            e = jnp.exp(s - top)
            e_self = jnp.exp(s_self - top)
            inv = 1.0 / (jnp.sum(e, axis=-1, keepdims=True) + e_self)
            p = (e * inv).astype(BF16)
            self_out = (e_self * inv).astype(BF16).astype(F32) * v3[rows, :]
            kcopy(c)[1].wait()
            outs = []
            for i in range(CHUNK // 2):
                vals = jnp.concatenate([vbuf[slot, 2 * i], vbuf[slot, 2 * i + 1]], 1)
                o = jnp.dot(p[16 * i:16 * i + 16], vals, preferred_element_type=F32)
                outs += [o[0:8, 0:HD], o[8:16, HD:2 * HD]]
            o3[rows, :] = jnp.concatenate(outs, 0) + self_out

            @pl.when(c + SLOTS < LAYERS * CHUNKS)
            def _():
                for cp in kcopy(c + SLOTS):
                    cp.start()
            return carry

        lax.fori_loop(0, CHUNKS, chunk_step, 0)
        attn = jnp.concatenate([o3[pl.ds(j, ROWS, stride=8), :] for j in range(HEADS)], 1).astype(BF16)
        wcopy(layer)[1].wait()
        proj = jnp.dot(attn, outw[wslot], preferred_element_type=F32)
        mid = (xbuf[layer].astype(F32) + proj).astype(BF16)

        @pl.when(me != layer)
        def _():
            hbuf[layer] = mid
            send_h(layer).start()

        @pl.when(layer + 1 < LAYERS)
        def _():
            for cp in wcopy(layer + 1):
                cp.start()

        @pl.when(me == layer)
        def _():
            hg[me] = mid
            gain = gf[pl.ds(layer, 1), :]

            @pl.when(layer == layer)
            def _():
                for cp in fcopy():
                    cp.wait()

            def half_step(turn, carry):
                half = (me // 2 + turn) % 2
                for k in range(2):
                    src = half * 2 + k

                    @pl.when(src != me)
                    def _():
                        recv_h(src).wait_recv()
                two = pl.ds(half * 2, 2)
                rows_h = hg[two].reshape(2 * ROWS, D)
                n2 = rms(rows_h, gain)
                for b in range(FFN // FBLK):
                    cols = slice(b * FBLK, (b + 1) * FBLK)
                    a = jnp.dot(n2, fg[:, cols], preferred_element_type=F32)
                    u = jnp.dot(n2, fu[:, cols], preferred_element_type=F32)
                    zbuf[:, cols] = (a * jax.nn.sigmoid(a) * u).astype(BF16)
                down = jnp.dot(zbuf[...], fd[...], preferred_element_type=F32)
                xg[two] = (rows_h.astype(F32) + down).astype(BF16).reshape(2, ROWS, D)
                for k in range(2):
                    dst = half * 2 + k

                    @pl.when(dst != me)
                    def _():
                        send_x(layer, dst).start()
                return carry

            lax.fori_loop(0, 2, half_step, 0)
            xbuf[layer + 1] = xg[me]

        @pl.when(me != layer)
        def _():
            send_h(layer).wait_send()
            send_x(layer, me).wait_recv()
        return carry

    lax.fori_loop(0, LAYERS, layer_step, 0)
    for step in range(1, 4):
        send_x(0, (me + step) % 4).wait_send()
    out[...] = xbuf[LAYERS]


def solution(mesh):
    row_spec = P(('grp', 'data'), None)
    rep_spec = P()
    cache_spec = P(None, ('grp', 'data'))
    len_spec = P(('grp', 'data'))
    owned_spec = P('data')

    def per_device(hidden, w_qkv, w_out, norm_attn, norm_ffn, k_cache, v_cache, seq_lens, w_gate, w_up, w_down):
        kc = k_cache.reshape(LAYERS, ROWS, 2 * CACHE, HD)
        vc = v_cache.reshape(LAYERS, ROWS, 2 * CACHE, HD)
        vm = pl.BlockSpec(memory_space=pltpu.VMEM)
        anys = pl.BlockSpec(memory_space=pl.ANY)
        dma = pltpu.SemaphoreType.DMA
        return pl.pallas_call(
            kernel,
            out_shape=jax.ShapeDtypeStruct((ROWS, D), BF16),
            in_specs=[vm] * 4 + [anys] * 7,
            out_specs=vm,
            scratch_shapes=[
                pltpu.VMEM((SLOTS, CHUNK, 2 * CACHE, HD), BF16),
                pltpu.VMEM((SLOTS, CHUNK, 2 * CACHE, HD), BF16),
                pltpu.VMEM((2, D, QKV), BF16),
                pltpu.VMEM((2, D, D), BF16),
                pltpu.VMEM((D, FFN), BF16),
                pltpu.VMEM((D, FFN), BF16),
                pltpu.VMEM((FFN, D), BF16),
                pltpu.VMEM((ROWS * 8, HD), F32),
                pltpu.VMEM((ROWS * 8, HD), F32),
                pltpu.VMEM((ROWS * 8, HD), F32),
                pltpu.VMEM((ROWS * 8, HD), F32),
                pltpu.VMEM((ROWS * 8, HD), F32),
                pltpu.VMEM((LAYERS + 1, ROWS, D), BF16),
                pltpu.VMEM((LAYERS, ROWS, D), BF16),
                pltpu.VMEM((4, ROWS, D), BF16),
                pltpu.VMEM((4, ROWS, D), BF16),
                pltpu.VMEM((2 * ROWS, FFN), BF16),
                dma((SLOTS,)), dma((SLOTS,)), dma((2, 2)), dma((3,)),
                dma((LAYERS,)), dma((4,)), dma((4,)), dma((LAYERS,)),
            ],
            compiler_params=pltpu.CompilerParams(collective_id=0, has_side_effects=True, vmem_limit_bytes=67043328),
        )(hidden, norm_attn, norm_ffn, seq_lens.reshape(1, ROWS), w_qkv, w_out, kc, vc, w_gate, w_up, w_down)

    return jax.shard_map(per_device, mesh=mesh, in_specs=(row_spec, rep_spec, rep_spec, rep_spec, rep_spec, cache_spec, cache_spec, len_spec, owned_spec, owned_spec, owned_spec), out_specs=row_spec, check_vma=False)
```

time: 464 us -> 76.2 us (0.16)
  local copies, waits for them, and re-layouts: 145 us -> 1.54 us
  other arithmetic: 105 us -> 0 us
  waiting for transfers between devices: 96.5 us -> 0 us
  Pallas kernels: 0 us -> 74.4 us
  matrix products: 62.4 us -> 0 us
  blocking collectives: 24.6 us -> 0 us
  starting transfers between devices: 14.1 us -> 0 us
  between operations: 13.1 us -> 0.01 us
    unnamed x3 -> x0, other arithmetic: 98.2 us -> none
    unnamed x19 -> x1, local copies, waits for them, and re-layouts: 82.8 us -> 1.54 us
    reduce_scatter x4 -> x0, waiting for transfers between devices: 80.2 us -> none  [layer_step(): lax.psum_scatter(partial_out, 'data', scatter_dimension=0, tiled=True)]
    pallas_call x0 -> x1, Pallas kernels: none -> 74.4 us  [per_device(): pl.pallas_call(kernel, out_shape=jax.ShapeDtypeStruct((ROWS, D), BF16), i...]
    dot_general x28 -> x0, matrix products: 62.4 us -> none  [the longest x4 18.6 us: attention_block(): jnp.einsum('bkgs,bskd->bkgd', p_cache, layer_vals, preferred_element_type...]
    dynamic_slice x8 -> x0, local copies, waits for them, and re-layouts: 58.9 us -> none  [per_device(): lax.scan(layer_step, hidden, (w_qkv, w_out, norm_attn, norm_ffn, k_cache,...]
    all_gather x4 -> x0, blocking collectives: 24.6 us -> none  [layer_step(): all_normed = lax.all_gather(normed, 'data', axis=0, tiled=True)]
    all_to_all x3 -> x0, waiting for transfers between devices: 16.3 us -> none  [the longest x1 16.3 us: per_device(): gate_cols = lax.all_to_all(w_gate, 'data', 2, 0, tiled=True)]
  transfers between devices with their start and end apart: 7 -> 0, of which waited for: 5 -> 0; matrix products, arithmetic and copies ran while one was open for 26% -> 0% of each run, Pallas kernels for 0% -> 0%
where the time goes in v1:
time: 76.2 us; the launch traced here: 75.9 us
  Pallas kernels  74.4 us (98%)
  local copies, waits for them, and re-layouts  1.54 us (2%)
    pallas_call x1, Pallas kernels, per_device(): pl.pallas_call(kernel, out_shape=jax.ShapeDtypeStruct((ROWS, D), BF16), i...  74.4 us
    unnamed x1, local copies, waits for them, and re-layouts  1.54 us

profile of v1, /device:TPU:0, one launch (start us, length us, event | category | flops | bytes accessed | tf_op | source)
XLA Modules:
  0.0 75.9 jit_solution(4996714203445709935)
XLA Ops:
  0.0 74.4 %shard_map.109 = bf16[64,768]{1,0:T(8,128)(2,1)} custom-call(bf16[64,768]{1,0:T(8,128)(2,1)} %hid.1, f32[4,768]{1,0:T(4,128)} %ga.1, f32[4,768]{1,0:T(4,128)} %gf.1, s32[1,64]{1,0:T(1,128)} %bitcast.5, bf16[4,768,1280]{2,1,0:T(8,128)(2,1)} %wqkv.1, bf16[4,768,768]{2,1,0:T(8,128)(2,1)} %wout.1, bf16[4,64,512,128]{3,2,1,0:T(8,128)(2,1)} %bitcast.3, ...), custom_call_target="tpu_custom_call" | custom-call | tf_op jit(solution)/shard_map/pallas_call | solution.py:228
  74.4 1.5 %copy.13 = bf16[64,768]{1,0:T(8,128)(2,1)} copy(bf16[64,768]{1,0:T(8,128)(2,1)} %shard_map.109) | data formatting | bytes 196608

commit v2 on v1

v2 whole, which is shorter than its diff:
```python
import jax
import jax.numpy as jnp
from jax import lax
from jax.experimental import pallas as pl
from jax.experimental.pallas import tpu as pltpu
from jax.sharding import PartitionSpec as P

NORM_EPS = 1e-5
F32 = jnp.float32
BF16 = jnp.bfloat16
LAYERS = 4
ROWS = 64
D = 768
HD = 128
HEADS = 6
CACHE = 256
QKV = 1280
FFN = 2048
CHUNK = 16
CHUNKS = ROWS // CHUNK
SLOTS = 6
HALF = ROWS // 2
FBLK = 512
NT = (((1,), (1,)), ((), ()))


def rms(rows_bf16, gain):
    vals = rows_bf16.astype(F32)
    inv = lax.rsqrt(jnp.mean(vals * vals, axis=-1, keepdims=True) + NORM_EPS)
    return (vals * inv * gain).astype(BF16)


def kernel(hid, ga, gf, lens, wqkv, wout, kc, vc, wg, wu, wd, out,
           kbuf, vbuf, qkvw, outw, fg, fu, fd, q3, k3, v3, o3, len3, xbuf, hbuf, hin, xo, zbuf,
           ksem, vsem, wsem, fsem, fs_sem, fr_sem, hs_sem, hr_sem, xs_sem, xr_sem):
    me = lax.axis_index("data")
    chip, core = me // 2, me % 2
    mate, peer = chip * 2 + (1 - core), (me + 2) % 4
    mesh_id = pl.DeviceIdType.MESH

    def kcopy(c, which):
        layer, part, slot = c // CHUNKS, c % CHUNKS, c % SLOTS
        src = pl.ds(pl.multiple_of(part * CHUNK, CHUNK), CHUNK)
        if which == 0:
            return pltpu.make_async_copy(kc.at[layer, src], kbuf.at[slot], ksem.at[slot])
        return pltpu.make_async_copy(vc.at[layer, src], vbuf.at[slot], vsem.at[slot])

    def wcopy(layer, which):
        slot = layer % 2
        if which == 0:
            return pltpu.make_async_copy(wqkv.at[layer], qkvw.at[slot], wsem.at[slot, 0])
        return pltpu.make_async_copy(wout.at[layer], outw.at[slot], wsem.at[slot, 1])

    ffn_parts = ((wg, fg), (wu, fu), (wd, fd))

    def fcopy(k):
        return pltpu.make_async_copy(ffn_parts[k][0].at[0], ffn_parts[k][1].at[core], fsem.at[k])

    def fsend(k, idx):
        return pltpu.make_async_remote_copy(
            src_ref=ffn_parts[k][0].at[0], dst_ref=ffn_parts[k][1].at[idx], send_sem=fs_sem.at[k], recv_sem=fr_sem.at[k],
            device_id={"data": mate}, device_id_type=mesh_id)

    def send_h(layer, half, dst, slot, pos):
        rows = pl.ds(pl.multiple_of(half * HALF, HALF), HALF)
        return pltpu.make_async_remote_copy(
            src_ref=hbuf.at[layer, rows], dst_ref=hin.at[slot, pos, rows],
            send_sem=hs_sem.at[layer, half], recv_sem=hr_sem.at[slot, pos, half],
            device_id={"data": dst}, device_id_type=mesh_id)

    def send_x(layer, dst, slot, pos):
        return pltpu.make_async_remote_copy(
            src_ref=xo.at[slot, pos], dst_ref=xbuf.at[layer + 1], send_sem=xs_sem.at[slot, pos], recv_sem=xr_sem.at[layer],
            device_id={"data": dst}, device_id_type=mesh_id)

    wcopy(0, 0).start()
    for c in range(CHUNKS):
        for which in range(2):
            kcopy(c, which).start()
    wcopy(0, 1).start()
    for k in range(3):
        fcopy(k).start()
    for c in range(CHUNKS, SLOTS):
        for which in range(2):
            kcopy(c, which).start()

    barrier = pltpu.get_barrier_semaphore()
    for step in range(1, 4):
        pl.semaphore_signal(barrier, inc=1, device_id={"data": (me + step) % 4}, device_id_type=mesh_id)
    pl.semaphore_wait(barrier, 3)

    @pl.when(me != 0)
    def _():
        for k in range(3):
            fsend(k, core).start()

    pick = (lax.broadcasted_iota(jnp.int32, (ROWS * 8, ROWS), 0) // 8 == lax.broadcasted_iota(jnp.int32, (ROWS * 8, ROWS), 1))
    lrow = jnp.broadcast_to(lens[...].astype(F32), (HD, ROWS)).astype(BF16)
    len3[...] = 2.0 * lax.dot_general(pick.astype(F32).astype(BF16), lrow, NT, preferred_element_type=F32)
    zrow = jnp.zeros((ROWS, HD), F32)
    for j in (6, 7):
        for ref in (q3, k3, v3):
            ref[pl.ds(j, ROWS, stride=8), :] = zrow
    xbuf[0] = hid[...]

    def is_local(layer):
        return (chip == layer // 2) & ((layer > 0) | (me == 0))

    def layer_step(layer, carry):
        wslot = layer % 2
        local = is_local(layer)
        dst = jnp.where(layer == 0, 0, peer)
        slot = jnp.where((layer == 0) & (me == 1), 0, 2 * (layer % 2) + 1)
        pos = jnp.where(layer == 0, core, 0)
        wcopy(layer, 0).wait()

        @pl.when((layer > 0) & jnp.logical_not(is_local(layer - 1)))
        def _():
            send_x(layer - 1, me, 0, 0).wait_recv()

        normed = rms(xbuf[layer], ga[pl.ds(layer, 1), :])
        qkv = jnp.dot(normed, qkvw[wslot], preferred_element_type=F32).astype(BF16).astype(F32)
        for j in range(HEADS):
            rows8 = pl.ds(j, ROWS, stride=8)
            kv = j * 2 // HEADS
            q3[rows8, :] = qkv[:, j * HD:(j + 1) * HD]
            k3[rows8, :] = qkv[:, (HEADS + kv) * HD:(HEADS + kv + 1) * HD]
            v3[rows8, :] = qkv[:, (HEADS + 2 + kv) * HD:(HEADS + 3 + kv) * HD]

        def chunk_step(part, carry):
            c = layer * CHUNKS + part
            cslot = c % SLOTS
            base = pl.multiple_of(part * (CHUNK * 8), CHUNK * 8)
            rows = pl.ds(base, CHUNK * 8)
            qc = q3[rows, :]
            s_self = jnp.sum(qc * k3[rows, :], axis=-1, keepdims=True) * (HD ** -0.5)
            kcopy(c, 0).wait()
            zero = jnp.zeros((8, HD), F32)
            scores = []
            for i in range(CHUNK // 2):
                qa = qc[16 * i:16 * i + 8]
                qb = qc[16 * i + 8:16 * i + 16]
                lhs = jnp.concatenate([jnp.concatenate([qa, zero], 1), jnp.concatenate([zero, qb], 1)], 0).astype(BF16)
                keys = jnp.concatenate([kbuf[cslot, 2 * i], kbuf[cslot, 2 * i + 1]], 1)
                scores.append(lax.dot_general(lhs, keys, NT, preferred_element_type=F32))
            s = jnp.concatenate(scores, 0) * (HD ** -0.5)
            col = lax.broadcasted_iota(jnp.int32, s.shape, 1)
            head = lax.broadcasted_iota(jnp.int32, s.shape, 0) % 8
            lim = len3[rows, :]
            lim = jnp.concatenate([lim] * (2 * CACHE // HD), 1)
            good = (col % 2 == head // 3) & (col.astype(F32) < lim)
            s = jnp.where(good, s, -1e30)
            top = jnp.maximum(jnp.max(s, axis=-1, keepdims=True), s_self)
            e = jnp.exp(s - top)
            e_self = jnp.exp(s_self - top)
            inv = 1.0 / (jnp.sum(e, axis=-1, keepdims=True) + e_self)
            p = (e * inv).astype(BF16)
            self_out = (e_self * inv).astype(BF16).astype(F32) * v3[rows, :]
            kcopy(c, 1).wait()
            outs = []
            for i in range(CHUNK // 2):
                vals = jnp.concatenate([vbuf[cslot, 2 * i], vbuf[cslot, 2 * i + 1]], 1)
                o = jnp.dot(p[16 * i:16 * i + 16], vals, preferred_element_type=F32)
                outs += [o[0:8, 0:HD], o[8:16, HD:2 * HD]]
            o3[rows, :] = jnp.concatenate(outs, 0) + self_out

            @pl.when(c + SLOTS < LAYERS * CHUNKS)
            def _():
                for which in range(2):
                    kcopy(c + SLOTS, which).start()
            return carry

        def half_att(half, carry):
            lax.fori_loop(half * (CHUNKS // 2), (half + 1) * (CHUNKS // 2), chunk_step, 0)

            @pl.when(half == 0)
            def _():
                wcopy(layer, 1).wait()

            base = half * (HALF * 8)
            attn = jnp.concatenate([o3[pl.ds(base + j, HALF, stride=8), :] for j in range(HEADS)], 1).astype(BF16)
            proj = jnp.dot(attn, outw[wslot], preferred_element_type=F32)
            rows = pl.ds(pl.multiple_of(half * HALF, HALF), HALF)
            mid = (xbuf[layer, rows].astype(F32) + proj).astype(BF16)

            @pl.when(local)
            def _():
                hin[2 * (layer % 2), 0, rows] = mid

            @pl.when(jnp.logical_not(local))
            def _():
                hbuf[layer, rows] = mid
                send_h(layer, half, dst, slot, pos).start()
            return carry

        lax.fori_loop(0, 2, half_att, 0)

        @pl.when(layer + 1 < LAYERS)
        def _():
            for which in range(2):
                wcopy(layer + 1, which).start()

        def ffn_step(turn, carry):
            serve = chip == turn
            tl = jnp.where(serve, jnp.where(chip == 0, layer - 1, layer + 1), layer)
            todo = jnp.where(serve, (layer >= 1) & (layer <= 2), tl // 2 == chip) & ((tl > 0) | (me == 0))

            @pl.when(todo)
            def _():
                idx = tl % 2
                fslot = 2 * idx + jnp.where(serve, 1, 0)
                both = tl == 0

                @pl.when(serve)
                def _():
                    for half in range(2):
                        send_h(0, half, me, fslot, 0).wait_recv()

                @pl.when(both)
                def _():
                    for half in range(2):
                        send_h(0, half, me, fslot, 1).wait_recv()

                first = jnp.where(serve, 1, 0) == chip

                @pl.when(first & (idx == core))
                def _():
                    for k in range(3):
                        fcopy(k).wait()

                @pl.when(first & (idx != core))
                def _():
                    for k in range(3):
                        fsend(k, idx).wait_recv()

                rows_h = hin[fslot].reshape(2 * ROWS, D)
                n2 = rms(rows_h, gf[pl.ds(tl, 1), :])
                for b in range(FFN // FBLK):
                    cols = slice(b * FBLK, (b + 1) * FBLK)
                    a = jnp.dot(n2, fg[idx, :, cols], preferred_element_type=F32)
                    u = jnp.dot(n2, fu[idx, :, cols], preferred_element_type=F32)
                    zbuf[:, cols] = (a * jax.nn.sigmoid(a) * u).astype(BF16)
                down = jnp.dot(zbuf[...], fd[idx], preferred_element_type=F32)
                xo[fslot] = (rows_h.astype(F32) + down).astype(BF16).reshape(2, ROWS, D)

                @pl.when(serve)
                def _():
                    send_x(tl, peer, fslot, 0).start()

                @pl.when(jnp.logical_not(serve))
                def _():
                    xbuf[tl + 1] = xo[fslot, 0]

                @pl.when(both)
                def _():
                    send_x(tl, jnp.where(serve, 3, 1), fslot, 1).start()
            return carry

        lax.fori_loop(0, 2, ffn_step, 0)
        return carry

    lax.fori_loop(0, LAYERS, layer_step, 0)

    @pl.when(chip == 0)
    def _():
        send_x(LAYERS - 1, me, 0, 0).wait_recv()

    out[...] = xbuf[LAYERS]

    for layer in range(LAYERS):
        @pl.when(jnp.logical_not(is_local(layer)))
        def _():
            for half in range(2):
                send_h(layer, half, 0, 0, 0).wait_send()

    @pl.when(me != 0)
    def _():
        send_x(0, me, 3, 0).wait_send()
        for k in range(3):
            fsend(k, core).wait_send()

    @pl.when(chip == 1)
    def _():
        send_x(0, me, 1, 0).wait_send()

    @pl.when(me == 0)
    def _():
        for slot, pos in ((0, 1), (1, 0), (1, 1), (3, 0)):
            send_x(0, me, slot, pos).wait_send()


def solution(mesh):
    row_spec = P(('grp', 'data'), None)
    rep_spec = P()
    cache_spec = P(None, ('grp', 'data'))
    len_spec = P(('grp', 'data'))
    owned_spec = P('data')

    def per_device(hidden, w_qkv, w_out, norm_attn, norm_ffn, k_cache, v_cache, seq_lens, w_gate, w_up, w_down):
        kc = k_cache.reshape(LAYERS, ROWS, 2 * CACHE, HD)
        vc = v_cache.reshape(LAYERS, ROWS, 2 * CACHE, HD)
        vm = pl.BlockSpec(memory_space=pltpu.VMEM)
        anys = pl.BlockSpec(memory_space=pl.ANY)
        dma = pltpu.SemaphoreType.DMA
        return pl.pallas_call(
            kernel,
            out_shape=jax.ShapeDtypeStruct((ROWS, D), BF16),
            in_specs=[vm] * 4 + [anys] * 7,
            out_specs=vm,
            scratch_shapes=[
                pltpu.VMEM((SLOTS, CHUNK, 2 * CACHE, HD), BF16),
                pltpu.VMEM((SLOTS, CHUNK, 2 * CACHE, HD), BF16),
                pltpu.VMEM((2, D, QKV), BF16),
                pltpu.VMEM((2, D, D), BF16),
                pltpu.VMEM((2, D, FFN), BF16),
                pltpu.VMEM((2, D, FFN), BF16),
                pltpu.VMEM((2, FFN, D), BF16),
                pltpu.VMEM((ROWS * 8, HD), F32),
                pltpu.VMEM((ROWS * 8, HD), F32),
                pltpu.VMEM((ROWS * 8, HD), F32),
                pltpu.VMEM((ROWS * 8, HD), F32),
                pltpu.VMEM((ROWS * 8, HD), F32),
                pltpu.VMEM((LAYERS + 1, ROWS, D), BF16),
                pltpu.VMEM((LAYERS, ROWS, D), BF16),
                pltpu.VMEM((4, 2, ROWS, D), BF16),
                pltpu.VMEM((4, 2, ROWS, D), BF16),
                pltpu.VMEM((2 * ROWS, FFN), BF16),
                dma((SLOTS,)), dma((SLOTS,)), dma((2, 2)), dma((3,)), dma((3,)), dma((3,)),
                dma((LAYERS, 2)), dma((4, 2, 2)), dma((4, 2)), dma((LAYERS,)),
            ],
            compiler_params=pltpu.CompilerParams(collective_id=0, has_side_effects=True, vmem_limit_bytes=67043328),
        )(hidden, norm_attn, norm_ffn, seq_lens.reshape(1, ROWS), w_qkv, w_out, kc, vc, w_gate, w_up, w_down)

    return jax.shard_map(per_device, mesh=mesh, in_specs=(row_spec, rep_spec, rep_spec, rep_spec, rep_spec, cache_spec, cache_spec, len_spec, owned_spec, owned_spec, owned_spec), out_specs=row_spec, check_vma=False)
```

time: 76.2 us -> 66.4 us (0.87)
  the two profiles are of different devices: /device:TPU:0 before, /device:TPU:6 now
where the time goes in v2:
time: 66.4 us; the launch traced here: 66.2 us
  Pallas kernels  64.7 us (97%)
  local copies, waits for them, and re-layouts  1.54 us (2%)
    pallas_call x1, Pallas kernels, per_device(): pl.pallas_call(kernel, out_shape=jax.ShapeDtypeStruct((ROWS, D), BF16), i...  64.7 us
    unnamed x1, local copies, waits for them, and re-layouts  1.54 us

profile of v2, /device:TPU:6, one launch (start us, length us, event | category | flops | bytes accessed | tf_op | source)
XLA Modules:
  0.0 66.2 jit_solution(8316735444028732890)
XLA Ops:
  0.0 64.7 %shard_map.109 = bf16[64,768]{1,0:T(8,128)(2,1)} custom-call(bf16[64,768]{1,0:T(8,128)(2,1)} %hid.1, f32[4,768]{1,0:T(4,128)} %ga.1, f32[4,768]{1,0:T(4,128)} %gf.1, s32[1,64]{1,0:T(1,128)} %bitcast.5, bf16[4,768,1280]{2,1,0:T(8,128)(2,1)} %wqkv.1, bf16[4,768,768]{2,1,0:T(8,128)(2,1)} %wout.1, bf16[4,64,512,128]{3,2,1,0:T(8,128)(2,1)} %bitcast.3, ...), custom_call_target="tpu_custom_call" | custom-call | tf_op jit(solution)/shard_map/pallas_call | solution.py:305
  64.7 1.5 %copy.13 = bf16[64,768]{1,0:T(8,128)(2,1)} copy(bf16[64,768]{1,0:T(8,128)(2,1)} %shard_map.109) | data formatting | bytes 196608

commit v3 on v2

--- a/solution.py
+++ b/solution.py
@@ -30,9 +30,9 @@
     return (vals * inv * gain).astype(BF16)
 
 
-def kernel(hid, ga, gf, lens, wqkv, wout, kc, vc, wg, wu, wd, out,
+def kernel(hid_in, ga_in, gf_in, lens_in, wqkv, wout, kc, vc, wg, wu, wd, out,
            kbuf, vbuf, qkvw, outw, fg, fu, fd, q3, k3, v3, o3, len3, xbuf, hbuf, hin, xo, zbuf,
-           ksem, vsem, wsem, fsem, fs_sem, fr_sem, hs_sem, hr_sem, xs_sem, xr_sem):
+           ksem, vsem, wsem, fsem, fs_sem, fr_sem, hs_sem, hr_sem, xs_sem, xr_sem, ga, gf, lens, isem):
     me = lax.axis_index("data")
     chip, core = me // 2, me % 2
     mate, peer = chip * 2 + (1 - core), (me + 2) % 4
@@ -73,26 +73,20 @@
             src_ref=xo.at[slot, pos], dst_ref=xbuf.at[layer + 1], send_sem=xs_sem.at[slot, pos], recv_sem=xr_sem.at[layer],
             device_id={"data": dst}, device_id_type=mesh_id)
 
+    small = [pltpu.make_async_copy(src, dst, isem.at[k]) for k, (src, dst) in enumerate(
+        ((hid_in, xbuf.at[0]), (ga_in, ga), (gf_in, gf), (lens_in, lens)))]
+    for cp in small:
+        cp.start()
     wcopy(0, 0).start()
-    for c in range(CHUNKS):
-        for which in range(2):
-            kcopy(c, which).start()
-    wcopy(0, 1).start()
-    for k in range(3):
-        fcopy(k).start()
-    for c in range(CHUNKS, SLOTS):
+    for c in range(3):
         for which in range(2):
             kcopy(c, which).start()
 
     barrier = pltpu.get_barrier_semaphore()
     for step in range(1, 4):
         pl.semaphore_signal(barrier, inc=1, device_id={"data": (me + step) % 4}, device_id_type=mesh_id)
-    pl.semaphore_wait(barrier, 3)
-
-    @pl.when(me != 0)
-    def _():
-        for k in range(3):
-            fsend(k, core).start()
+    for cp in small:
+        cp.wait()
 
     pick = (lax.broadcasted_iota(jnp.int32, (ROWS * 8, ROWS), 0) // 8 == lax.broadcasted_iota(jnp.int32, (ROWS * 8, ROWS), 1))
     lrow = jnp.broadcast_to(lens[...].astype(F32), (HD, ROWS)).astype(BF16)
@@ -101,7 +95,7 @@
     for j in (6, 7):
         for ref in (q3, k3, v3):
             ref[pl.ds(j, ROWS, stride=8), :] = zrow
-    xbuf[0] = hid[...]
+    pl.semaphore_wait(barrier, 3)
 
     def is_local(layer):
         return (chip == layer // 2) & ((layer > 0) | (me == 0))
@@ -132,6 +126,28 @@
             cslot = c % SLOTS
             base = pl.multiple_of(part * (CHUNK * 8), CHUNK * 8)
             rows = pl.ds(base, CHUNK * 8)
+
+            @pl.when((layer > 0) & (c + SLOTS - 1 < LAYERS * CHUNKS))
+            def _():
+                for which in range(2):
+                    kcopy(c + SLOTS - 1, which).start()
+
+            @pl.when(c == 0)
+            def _():
+                for which in range(2):
+                    kcopy(3, which).start()
+                wcopy(0, 1).start()
+
+            @pl.when(c == jnp.where(chip == 0, 1, CHUNKS + 1))
+            def _():
+                for k in range(3):
+                    fcopy(k).start()
+
+            @pl.when(c == 3)
+            def _():
+                for which in range(2):
+                    kcopy(4, which).start()
+
             qc = q3[rows, :]
             s_self = jnp.sum(qc * k3[rows, :], axis=-1, keepdims=True) * (HD ** -0.5)
             kcopy(c, 0).wait()
@@ -163,11 +179,6 @@
                 o = jnp.dot(p[16 * i:16 * i + 16], vals, preferred_element_type=F32)
                 outs += [o[0:8, 0:HD], o[8:16, HD:2 * HD]]
             o3[rows, :] = jnp.concatenate(outs, 0) + self_out
-
-            @pl.when(c + SLOTS < LAYERS * CHUNKS)
-            def _():
-                for which in range(2):
-                    kcopy(c + SLOTS, which).start()
             return carry
 
         def half_att(half, carry):
@@ -200,10 +211,25 @@
             for which in range(2):
                 wcopy(layer + 1, which).start()
 
+        @pl.when(layer == 0)
+        def _():
+            for c in range(CHUNKS + 1, CHUNKS + SLOTS - 1):
+                for which in range(2):
+                    kcopy(c, which).start()
+
+        @pl.when((layer == 0) & (me != 0))
+        def _():
+            for k in range(3):
+                fsend(k, core).start()
+
         def ffn_step(turn, carry):
-            serve = chip == turn
-            tl = jnp.where(serve, jnp.where(chip == 0, layer - 1, layer + 1), layer)
-            todo = jnp.where(serve, (layer >= 1) & (layer <= 2), tl // 2 == chip) & ((tl > 0) | (me == 0))
+            serve0 = (layer == 2) | (turn == 1)
+            serve1 = (layer != 2) & (turn == 0)
+            serve = jnp.where(chip == 0, serve0, serve1)
+            tl = jnp.where(chip == 0, jnp.where(layer == 2, 1, layer), jnp.where(layer == 1, 2, layer))
+            todo0 = jnp.where(turn == 0, layer < 3, layer == 0) & ((layer > 0) | (me == 0))
+            todo1 = jnp.where(turn == 0, layer > 0, layer == 3)
+            todo = jnp.where(chip == 0, todo0, todo1)
 
             @pl.when(todo)
             def _():
@@ -305,7 +331,7 @@
         return pl.pallas_call(
             kernel,
             out_shape=jax.ShapeDtypeStruct((ROWS, D), BF16),
-            in_specs=[vm] * 4 + [anys] * 7,
+            in_specs=[anys] * 11,
             out_specs=vm,
             scratch_shapes=[
                 pltpu.VMEM((SLOTS, CHUNK, 2 * CACHE, HD), BF16),
@@ -327,6 +353,7 @@
                 pltpu.VMEM((2 * ROWS, FFN), BF16),
                 dma((SLOTS,)), dma((SLOTS,)), dma((2, 2)), dma((3,)), dma((3,)), dma((3,)),
                 dma((LAYERS, 2)), dma((4, 2, 2)), dma((4, 2)), dma((LAYERS,)),
+                pltpu.VMEM((LAYERS, D), F32), pltpu.VMEM((LAYERS, D), F32), pltpu.VMEM((1, ROWS), jnp.int32), dma((4,)),
             ],
             compiler_params=pltpu.CompilerParams(collective_id=0, has_side_effects=True, vmem_limit_bytes=67043328),
         )(hidden, norm_attn, norm_ffn, seq_lens.reshape(1, ROWS), w_qkv, w_out, kc, vc, w_gate, w_up, w_down)

time: 66.4 us -> 62.1 us (0.935)
  the two profiles are of different devices: /device:TPU:6 before, /device:TPU:0 now
where the time goes in v3:
time: 62.1 us; the launch traced here: 62 us
  Pallas kernels  60.4 us (97%)
  local copies, waits for them, and re-layouts  1.54 us (2%)
    pallas_call x1, Pallas kernels, per_device(): pl.pallas_call(kernel, out_shape=jax.ShapeDtypeStruct((ROWS, D), BF16), i...  60.4 us
    unnamed x1, local copies, waits for them, and re-layouts  1.54 us

profile of v3, /device:TPU:0, one launch (start us, length us, event | category | flops | bytes accessed | tf_op | source)
XLA Modules:
  0.0 62.0 jit_solution(130607445128277160)
XLA Ops:
  0.0 60.4 %shard_map.109 = bf16[64,768]{1,0:T(8,128)(2,1)} custom-call(bf16[64,768]{1,0:T(8,128)(2,1)} %hid_in.1, f32[4,768]{1,0:T(4,128)} %ga_in.1, f32[4,768]{1,0:T(4,128)} %gf_in.1, s32[1,64]{1,0:T(1,128)} %bitcast.5, bf16[4,768,1280]{2,1,0:T(8,128)(2,1)} %wqkv.1, bf16[4,768,768]{2,1,0:T(8,128)(2,1)} %wout.1, bf16[4,64,512,128]{3,2,1,0:T(8,128)(2,1)} %bitcast.3, ...), custom_call_target="tpu_custom_call" | custom-call | tf_op jit(solution)/shard_map/pallas_call | solution.py:331
  60.4 1.5 %copy.13 = bf16[64,768]{1,0:T(8,128)(2,1)} copy(bf16[64,768]{1,0:T(8,128)(2,1)} %shard_map.109) | data formatting | bytes 196608

commit v4 on v3

--- a/solution.py
+++ b/solution.py
@@ -121,36 +121,41 @@
             k3[rows8, :] = qkv[:, (HEADS + kv) * HD:(HEADS + kv + 1) * HD]
             v3[rows8, :] = qkv[:, (HEADS + 2 + kv) * HD:(HEADS + 3 + kv) * HD]
 
-        def chunk_step(part, carry):
-            c = layer * CHUNKS + part
-            cslot = c % SLOTS
-            base = pl.multiple_of(part * (CHUNK * 8), CHUNK * 8)
-            rows = pl.ds(base, CHUNK * 8)
-
-            @pl.when((layer > 0) & (c + SLOTS - 1 < LAYERS * CHUNKS))
-            def _():
-                for which in range(2):
-                    kcopy(c + SLOTS - 1, which).start()
-
+        def issue_start(c):
             @pl.when(c == 0)
             def _():
                 for which in range(2):
                     kcopy(3, which).start()
                 wcopy(0, 1).start()
 
-            @pl.when(c == jnp.where(chip == 0, 1, CHUNKS + 1))
+            @pl.when((c == 0) & (me == 1))
+            def _():
+                for k in range(3):
+                    fsend(k, core).start()
+
+            @pl.when((c == jnp.where(chip == 0, 0, CHUNKS)) & (me != 1))
             def _():
                 for k in range(3):
                     fcopy(k).start()
 
-            @pl.when(c == 3)
-            def _():
-                for which in range(2):
-                    kcopy(4, which).start()
-
+        def issue_end(c):
+            @pl.when(c == 0)
+            def _():
+                for early in range(4, SLOTS):
+                    for which in range(2):
+                        kcopy(early, which).start()
+
+            @pl.when(c + SLOTS < LAYERS * CHUNKS)
+            def _():
+                for k in range(2):
+                    for which in range(2):
+                        kcopy(c + k + SLOTS, which).start()
+
+        def chunk_math(part):
+            cslot = (layer * CHUNKS + part) % SLOTS
+            rows = pl.ds(pl.multiple_of(part * (CHUNK * 8), CHUNK * 8), CHUNK * 8)
             qc = q3[rows, :]
             s_self = jnp.sum(qc * k3[rows, :], axis=-1, keepdims=True) * (HD ** -0.5)
-            kcopy(c, 0).wait()
             zero = jnp.zeros((8, HD), F32)
             scores = []
             for i in range(CHUNK // 2):
@@ -172,17 +177,24 @@
             inv = 1.0 / (jnp.sum(e, axis=-1, keepdims=True) + e_self)
             p = (e * inv).astype(BF16)
             self_out = (e_self * inv).astype(BF16).astype(F32) * v3[rows, :]
-            kcopy(c, 1).wait()
             outs = []
             for i in range(CHUNK // 2):
                 vals = jnp.concatenate([vbuf[cslot, 2 * i], vbuf[cslot, 2 * i + 1]], 1)
                 o = jnp.dot(p[16 * i:16 * i + 16], vals, preferred_element_type=F32)
                 outs += [o[0:8, 0:HD], o[8:16, HD:2 * HD]]
             o3[rows, :] = jnp.concatenate(outs, 0) + self_out
-            return carry
+
+        def chunk_pair(part):
+            issue_start(layer * CHUNKS + part)
+            for k in range(2):
+                for which in range(2):
+                    kcopy(layer * CHUNKS + part + k, which).wait()
+            for k in range(2):
+                chunk_math(part + k)
+            issue_end(layer * CHUNKS + part)
 
         def half_att(half, carry):
-            lax.fori_loop(half * (CHUNKS // 2), (half + 1) * (CHUNKS // 2), chunk_step, 0)
+            chunk_pair(half * (CHUNKS // 2))
 
             @pl.when(half == 0)
             def _():
@@ -211,16 +223,17 @@
             for which in range(2):
                 wcopy(layer + 1, which).start()
 
-        @pl.when(layer == 0)
-        def _():
-            for c in range(CHUNKS + 1, CHUNKS + SLOTS - 1):
-                for which in range(2):
-                    kcopy(c, which).start()
-
         @pl.when((layer == 0) & (me != 0))
         def _():
-            for k in range(3):
-                fsend(k, core).start()
+            @pl.when(me == 1)
+            def _():
+                for k in range(3):
+                    fcopy(k).start()
+
+            @pl.when(me != 1)
+            def _():
+                for k in range(3):
+                    fsend(k, core).start()
 
         def ffn_step(turn, carry):
             serve0 = (layer == 2) | (turn == 1)
@@ -259,15 +272,25 @@
                     for k in range(3):
                         fsend(k, idx).wait_recv()
 
-                rows_h = hin[fslot].reshape(2 * ROWS, D)
-                n2 = rms(rows_h, gf[pl.ds(tl, 1), :])
-                for b in range(FFN // FBLK):
-                    cols = slice(b * FBLK, (b + 1) * FBLK)
-                    a = jnp.dot(n2, fg[idx, :, cols], preferred_element_type=F32)
-                    u = jnp.dot(n2, fu[idx, :, cols], preferred_element_type=F32)
-                    zbuf[:, cols] = (a * jax.nn.sigmoid(a) * u).astype(BF16)
-                down = jnp.dot(zbuf[...], fd[idx], preferred_element_type=F32)
-                xo[fslot] = (rows_h.astype(F32) + down).astype(BF16).reshape(2, ROWS, D)
+                def ffn(count):
+                    rows_h = hin[fslot, 0:count].reshape(count * ROWS, D)
+                    n2 = rms(rows_h, gf[pl.ds(tl, 1), :])
+                    zrows = slice(0, count * ROWS)
+                    for b in range(FFN // FBLK):
+                        cols = slice(b * FBLK, (b + 1) * FBLK)
+                        a = jnp.dot(n2, fg[idx, :, cols], preferred_element_type=F32)
+                        u = jnp.dot(n2, fu[idx, :, cols], preferred_element_type=F32)
+                        zbuf[zrows, cols] = (a * jax.nn.sigmoid(a) * u).astype(BF16)
+                    down = jnp.dot(zbuf[zrows, :], fd[idx], preferred_element_type=F32)
+                    xo[fslot, 0:count] = (rows_h.astype(F32) + down).astype(BF16).reshape(count, ROWS, D)
+
+                @pl.when(both)
+                def _():
+                    ffn(2)
+
+                @pl.when(jnp.logical_not(both))
+                def _():
+                    ffn(1)
 
                 @pl.when(serve)
                 def _():

time: 62.1 us -> 62.9 us (1.013)
  Pallas kernels: 60.4 us -> 61.3 us
    pallas_call x1, Pallas kernels: 60.4 us -> 61.3 us  [per_device(): pl.pallas_call(kernel, out_shape=jax.ShapeDtypeStruct((ROWS, D), BF16), i...]
where the time goes in v4:
time: 62.9 us; the launch traced here: 62.8 us
  Pallas kernels  61.3 us (97%)
  local copies, waits for them, and re-layouts  1.54 us (2%)
    pallas_call x1, Pallas kernels, per_device(): pl.pallas_call(kernel, out_shape=jax.ShapeDtypeStruct((ROWS, D), BF16), i...  61.3 us
    unnamed x1, local copies, waits for them, and re-layouts  1.54 us

profile of v4, /device:TPU:0, one launch (start us, length us, event | category | flops | bytes accessed | tf_op | source)
XLA Modules:
  0.0 62.8 jit_solution(664230192347111826)
XLA Ops:
  0.0 61.3 %shard_map.109 = bf16[64,768]{1,0:T(8,128)(2,1)} custom-call(bf16[64,768]{1,0:T(8,128)(2,1)} %hid_in.1, f32[4,768]{1,0:T(4,128)} %ga_in.1, f32[4,768]{1,0:T(4,128)} %gf_in.1, s32[1,64]{1,0:T(1,128)} %bitcast.5, bf16[4,768,1280]{2,1,0:T(8,128)(2,1)} %wqkv.1, bf16[4,768,768]{2,1,0:T(8,128)(2,1)} %wout.1, bf16[4,64,512,128]{3,2,1,0:T(8,128)(2,1)} %bitcast.3, ...), custom_call_target="tpu_custom_call" | custom-call | tf_op jit(solution)/shard_map/pallas_call | solution.py:354
  61.3 1.5 %copy.13 = bf16[64,768]{1,0:T(8,128)(2,1)} copy(bf16[64,768]{1,0:T(8,128)(2,1)} %shard_map.109) | data formatting | bytes 196608

commit v5 on v4

--- a/solution.py
+++ b/solution.py
@@ -6,6 +6,7 @@
 from jax.sharding import PartitionSpec as P
 
 NORM_EPS = 1e-5
+EXP_SCALE = 1.4426950408889634 * 128 ** -0.5
 F32 = jnp.float32
 BF16 = jnp.bfloat16
 LAYERS = 4
@@ -34,19 +35,19 @@
            kbuf, vbuf, qkvw, outw, fg, fu, fd, q3, k3, v3, o3, len3, xbuf, hbuf, hin, xo, zbuf,
            ksem, vsem, wsem, fsem, fs_sem, fr_sem, hs_sem, hr_sem, xs_sem, xr_sem, ga, gf, lens, isem):
     me = lax.axis_index("data")
-    chip, core = me // 2, me % 2
-    mate, peer = chip * 2 + (1 - core), (me + 2) % 4
+    chip, core = lax.shift_right_logical(me, 1), lax.rem(me, 2)
+    mate, peer = chip * 2 + (1 - core), lax.rem(me + 2, 4)
     mesh_id = pl.DeviceIdType.MESH
 
     def kcopy(c, which):
-        layer, part, slot = c // CHUNKS, c % CHUNKS, c % SLOTS
+        layer, part, slot = lax.shift_right_logical(jnp.int32(c), 2), lax.rem(jnp.int32(c), CHUNKS), lax.rem(jnp.int32(c), SLOTS)
         src = pl.ds(pl.multiple_of(part * CHUNK, CHUNK), CHUNK)
         if which == 0:
             return pltpu.make_async_copy(kc.at[layer, src], kbuf.at[slot], ksem.at[slot])
         return pltpu.make_async_copy(vc.at[layer, src], vbuf.at[slot], vsem.at[slot])
 
     def wcopy(layer, which):
-        slot = layer % 2
+        slot = lax.rem(jnp.int32(layer), 2)
         if which == 0:
             return pltpu.make_async_copy(wqkv.at[layer], qkvw.at[slot], wsem.at[slot, 0])
         return pltpu.make_async_copy(wout.at[layer], outw.at[slot], wsem.at[slot, 1])
@@ -84,7 +85,7 @@
 
     barrier = pltpu.get_barrier_semaphore()
     for step in range(1, 4):
-        pl.semaphore_signal(barrier, inc=1, device_id={"data": (me + step) % 4}, device_id_type=mesh_id)
+        pl.semaphore_signal(barrier, inc=1, device_id={"data": lax.rem(me + step, 4)}, device_id_type=mesh_id)
     for cp in small:
         cp.wait()
 
@@ -97,14 +98,18 @@
             ref[pl.ds(j, ROWS, stride=8), :] = zrow
     pl.semaphore_wait(barrier, 3)
 
+    @pl.when(me != 0)
+    def _():
+        fsend(0, core).start()
+
     def is_local(layer):
         return (chip == layer // 2) & ((layer > 0) | (me == 0))
 
     def layer_step(layer, carry):
-        wslot = layer % 2
+        wslot = lax.rem(jnp.int32(layer), 2)
         local = is_local(layer)
         dst = jnp.where(layer == 0, 0, peer)
-        slot = jnp.where((layer == 0) & (me == 1), 0, 2 * (layer % 2) + 1)
+        slot = jnp.where((layer == 0) & (me == 1), 0, 2 * wslot + 1)
         pos = jnp.where(layer == 0, core, 0)
         wcopy(layer, 0).wait()
 
@@ -121,41 +126,21 @@
             k3[rows8, :] = qkv[:, (HEADS + kv) * HD:(HEADS + kv + 1) * HD]
             v3[rows8, :] = qkv[:, (HEADS + 2 + kv) * HD:(HEADS + 3 + kv) * HD]
 
-        def issue_start(c):
-            @pl.when(c == 0)
+        def refill(c, ok=True):
+            @pl.when((c < LAYERS * CHUNKS) & ok)
             def _():
                 for which in range(2):
-                    kcopy(3, which).start()
-                wcopy(0, 1).start()
-
-            @pl.when((c == 0) & (me == 1))
-            def _():
-                for k in range(3):
-                    fsend(k, core).start()
-
-            @pl.when((c == jnp.where(chip == 0, 0, CHUNKS)) & (me != 1))
-            def _():
-                for k in range(3):
-                    fcopy(k).start()
-
-        def issue_end(c):
-            @pl.when(c == 0)
-            def _():
-                for early in range(4, SLOTS):
-                    for which in range(2):
-                        kcopy(early, which).start()
-
-            @pl.when(c + SLOTS < LAYERS * CHUNKS)
-            def _():
-                for k in range(2):
-                    for which in range(2):
-                        kcopy(c + k + SLOTS, which).start()
+                    kcopy(c, which).start()
+
+        col8 = lax.broadcasted_iota(jnp.int32, (8, 2 * CACHE), 1)
+        kv8 = jnp.where(lax.broadcasted_iota(jnp.int32, (8, 2 * CACHE), 0) < HEADS // 2, 0, 1)
+        cols8 = jnp.where((col8 & 1) == kv8, col8.astype(F32), 4.0 * CACHE)[None]
 
         def chunk_math(part):
-            cslot = (layer * CHUNKS + part) % SLOTS
+            cslot = lax.rem(layer * CHUNKS + part, SLOTS)
             rows = pl.ds(pl.multiple_of(part * (CHUNK * 8), CHUNK * 8), CHUNK * 8)
             qc = q3[rows, :]
-            s_self = jnp.sum(qc * k3[rows, :], axis=-1, keepdims=True) * (HD ** -0.5)
+            s_self = jnp.sum(qc * k3[rows, :], axis=-1, keepdims=True).reshape(CHUNK, 8, 1)
             zero = jnp.zeros((8, HD), F32)
             scores = []
             for i in range(CHUNK // 2):
@@ -164,19 +149,15 @@
                 lhs = jnp.concatenate([jnp.concatenate([qa, zero], 1), jnp.concatenate([zero, qb], 1)], 0).astype(BF16)
                 keys = jnp.concatenate([kbuf[cslot, 2 * i], kbuf[cslot, 2 * i + 1]], 1)
                 scores.append(lax.dot_general(lhs, keys, NT, preferred_element_type=F32))
-            s = jnp.concatenate(scores, 0) * (HD ** -0.5)
-            col = lax.broadcasted_iota(jnp.int32, s.shape, 1)
-            head = lax.broadcasted_iota(jnp.int32, s.shape, 0) % 8
-            lim = len3[rows, :]
-            lim = jnp.concatenate([lim] * (2 * CACHE // HD), 1)
-            good = (col % 2 == head // 3) & (col.astype(F32) < lim)
-            s = jnp.where(good, s, -1e30)
+            s = jnp.concatenate(scores, 0).reshape(CHUNK, 8, 2 * CACHE)
+            lim = jnp.concatenate([len3[rows, :].reshape(CHUNK, 8, HD)] * (2 * CACHE // HD), 2)
+            s = jnp.where(cols8 < lim, s, -1e30 * HD ** 0.5)
             top = jnp.maximum(jnp.max(s, axis=-1, keepdims=True), s_self)
-            e = jnp.exp(s - top)
-            e_self = jnp.exp(s_self - top)
+            e = jnp.exp2((s - top) * EXP_SCALE)
+            e_self = jnp.exp2((s_self - top) * EXP_SCALE)
             inv = 1.0 / (jnp.sum(e, axis=-1, keepdims=True) + e_self)
-            p = (e * inv).astype(BF16)
-            self_out = (e_self * inv).astype(BF16).astype(F32) * v3[rows, :]
+            p = (e * inv).reshape(CHUNK * 8, 2 * CACHE).astype(BF16)
+            self_out = (e_self * inv).astype(BF16).astype(F32).reshape(CHUNK * 8, 1) * v3[rows, :]
             outs = []
             for i in range(CHUNK // 2):
                 vals = jnp.concatenate([vbuf[cslot, 2 * i], vbuf[cslot, 2 * i + 1]], 1)
@@ -185,15 +166,36 @@
             o3[rows, :] = jnp.concatenate(outs, 0) + self_out
 
         def chunk_pair(part):
-            issue_start(layer * CHUNKS + part)
             for k in range(2):
                 for which in range(2):
                     kcopy(layer * CHUNKS + part + k, which).wait()
             for k in range(2):
                 chunk_math(part + k)
-            issue_end(layer * CHUNKS + part)
 
         def half_att(half, carry):
+            @pl.when(half == 0)
+            def _():
+                @pl.when(layer == 0)
+                def _():
+                    for which in range(2):
+                        kcopy(3, which).start()
+                    wcopy(0, 1).start()
+
+                @pl.when(jnp.where(me == 0, layer == 0, (chip == 1) & (layer == 1)))
+                def _():
+                    for k in range(3):
+                        fcopy(k).start()
+
+            @pl.when(half == 1)
+            def _():
+                @pl.when(layer == 0)
+                def _():
+                    for c in (4, 5):
+                        for which in range(2):
+                            kcopy(c, which).start()
+
+                refill(layer * CHUNKS + 6)
+
             chunk_pair(half * (CHUNKS // 2))
 
             @pl.when(half == 0)
@@ -208,7 +210,7 @@
 
             @pl.when(local)
             def _():
-                hin[2 * (layer % 2), 0, rows] = mid
+                hin[2 * wslot, 0, rows] = mid
 
             @pl.when(jnp.logical_not(local))
             def _():
@@ -225,15 +227,15 @@
 
         @pl.when((layer == 0) & (me != 0))
         def _():
-            @pl.when(me == 1)
-            def _():
-                for k in range(3):
-                    fcopy(k).start()
-
-            @pl.when(me != 1)
-            def _():
-                for k in range(3):
-                    fsend(k, core).start()
+            for k in range(1, 3):
+                fsend(k, core).start()
+
+        @pl.when((layer == 0) & (me == 1))
+        def _():
+            for k in range(3):
+                fcopy(k).start()
+
+        refill(layer * CHUNKS + 7)
 
         def ffn_step(turn, carry):
             serve0 = (layer == 2) | (turn == 1)
@@ -246,7 +248,7 @@
 
             @pl.when(todo)
             def _():
-                idx = tl % 2
+                idx = lax.rem(tl, 2)
                 fslot = 2 * idx + jnp.where(serve, 1, 0)
                 both = tl == 0
 
@@ -305,7 +307,9 @@
                     send_x(tl, jnp.where(serve, 3, 1), fslot, 1).start()
             return carry
 
+        refill(layer * CHUNKS + 8)
         lax.fori_loop(0, 2, ffn_step, 0)
+        refill(layer * CHUNKS + 9)
         return carry
 
     lax.fori_loop(0, LAYERS, layer_step, 0)

time: 62.9 us -> 55.3 us (0.88)
  Pallas kernels: 61.3 us -> 53.6 us
    pallas_call x1, Pallas kernels: 61.3 us -> 53.6 us  [per_device(): pl.pallas_call(kernel, out_shape=jax.ShapeDtypeStruct((ROWS, D), BF16), i...]
where the time goes in v5:
time: 55.3 us; the launch traced here: 55.2 us
  Pallas kernels  53.6 us (97%)
  local copies, waits for them, and re-layouts  1.54 us (3%)
    pallas_call x1, Pallas kernels, per_device(): pl.pallas_call(kernel, out_shape=jax.ShapeDtypeStruct((ROWS, D), BF16), i...  53.6 us
    unnamed x1, local copies, waits for them, and re-layouts  1.54 us

profile of v5, /device:TPU:0, one launch (start us, length us, event | category | flops | bytes accessed | tf_op | source)
XLA Modules:
  0.0 55.2 jit_solution(16579774352712026307)
XLA Ops:
  0.0 53.6 %shard_map.109 = bf16[64,768]{1,0:T(8,128)(2,1)} custom-call(bf16[64,768]{1,0:T(8,128)(2,1)} %hid_in.1, f32[4,768]{1,0:T(4,128)} %ga_in.1, f32[4,768]{1,0:T(4,128)} %gf_in.1, s32[1,64]{1,0:T(1,128)} %bitcast.5, bf16[4,768,1280]{2,1,0:T(8,128)(2,1)} %wqkv.1, bf16[4,768,768]{2,1,0:T(8,128)(2,1)} %wout.1, bf16[4,64,512,128]{3,2,1,0:T(8,128)(2,1)} %bitcast.3, ...), custom_call_target="tpu_custom_call" | custom-call | tf_op jit(solution)/shard_map/pallas_call | solution.py:358
  53.6 1.5 %copy.13 = bf16[64,768]{1,0:T(8,128)(2,1)} copy(bf16[64,768]{1,0:T(8,128)(2,1)} %shard_map.109) | data formatting | bytes 196608

commit v6 on v5

--- a/solution.py
+++ b/solution.py
@@ -98,7 +98,7 @@
             ref[pl.ds(j, ROWS, stride=8), :] = zrow
     pl.semaphore_wait(barrier, 3)
 
-    @pl.when(me != 0)
+    @pl.when(me == 1)
     def _():
         fsend(0, core).start()
 
@@ -225,10 +225,17 @@
             for which in range(2):
                 wcopy(layer + 1, which).start()
 
+        @pl.when((layer == 0) & (chip == 1))
+        def _():
+            fsend(0, core).start()
+
         @pl.when((layer == 0) & (me != 0))
         def _():
-            for k in range(1, 3):
-                fsend(k, core).start()
+            fsend(1, core).start()
+
+        @pl.when(jnp.where(chip == 0, (layer == 0) & (me == 1), layer == 1))
+        def _():
+            fsend(2, core).start()
 
         @pl.when((layer == 0) & (me == 1))
         def _():
@@ -357,7 +364,7 @@
         dma = pltpu.SemaphoreType.DMA
         return pl.pallas_call(
             kernel,
-            out_shape=jax.ShapeDtypeStruct((ROWS, D), BF16),
+            out_shape=pltpu.VMEM((ROWS, D), BF16),
             in_specs=[anys] * 11,
             out_specs=vm,
             scratch_shapes=[
@@ -382,7 +389,7 @@
                 dma((LAYERS, 2)), dma((4, 2, 2)), dma((4, 2)), dma((LAYERS,)),
                 pltpu.VMEM((LAYERS, D), F32), pltpu.VMEM((LAYERS, D), F32), pltpu.VMEM((1, ROWS), jnp.int32), dma((4,)),
             ],
-            compiler_params=pltpu.CompilerParams(collective_id=0, has_side_effects=True, vmem_limit_bytes=67043328),
+            compiler_params=pltpu.CompilerParams(collective_id=0, has_side_effects=True, vmem_limit_bytes=64000000),
         )(hidden, norm_attn, norm_ffn, seq_lens.reshape(1, ROWS), w_qkv, w_out, kc, vc, w_gate, w_up, w_down)
 
     return jax.shard_map(per_device, mesh=mesh, in_specs=(row_spec, rep_spec, rep_spec, rep_spec, rep_spec, cache_spec, cache_spec, len_spec, owned_spec, owned_spec, owned_spec), out_specs=row_spec, check_vma=False)

time: 55.3 us -> 53.8 us (0.973)
  local copies, waits for them, and re-layouts: 1.54 us -> 0.64 us
  Pallas kernels: 53.6 us -> 53 us
    unnamed x1, local copies, waits for them, and re-layouts: 1.54 us -> 0.64 us
    pallas_call x1, Pallas kernels: 53.6 us -> 53 us  [per_device(): pl.pallas_call(kernel, out_shape=pltpu.VMEM((ROWS, D), BF16), in_specs=[a...]
where the time goes in v6:
time: 53.8 us; the launch traced here: 53.6 us
  Pallas kernels  53 us (99%)
  local copies, waits for them, and re-layouts  0.64 us (1%)
    pallas_call x1, Pallas kernels, per_device(): pl.pallas_call(kernel, out_shape=pltpu.VMEM((ROWS, D), BF16), in_specs=[a...  53 us

profile of v6, /device:TPU:0, one launch (start us, length us, event | category | flops | bytes accessed | tf_op | source)
XLA Modules:
  0.0 53.6 jit_solution(12669648949121589266)
XLA Ops:
  0.0 53.0 %shard_map.109 = bf16[64,768]{1,0:T(8,128)(2,1)S(1)} custom-call(bf16[64,768]{1,0:T(8,128)(2,1)} %hid_in.1, f32[4,768]{1,0:T(4,128)} %ga_in.1, f32[4,768]{1,0:T(4,128)} %gf_in.1, s32[1,64]{1,0:T(1,128)} %bitcast.5, bf16[4,768,1280]{2,1,0:T(8,128)(2,1)} %wqkv.1, bf16[4,768,768]{2,1,0:T(8,128)(2,1)} %wout.1, bf16[4,64,512,128]{3,2,1,0:T(8,128)(2,1)} %bitcast.3, ...), custom_call_target="tpu_custom_call" | custom-call | tf_op jit(solution)/shard_map/pallas_call | solution.py:365
  53.0 0.6 %copy.13 = bf16[64,768]{1,0:T(8,128)(2,1)} copy(bf16[64,768]{1,0:T(8,128)(2,1)S(1)} %shard_map.109) | data formatting | bytes 196608

commit v7 on v6

--- a/solution.py
+++ b/solution.py
@@ -69,9 +69,11 @@
             send_sem=hs_sem.at[layer, half], recv_sem=hr_sem.at[slot, pos, half],
             device_id={"data": dst}, device_id_type=mesh_id)
 
-    def send_x(layer, dst, slot, pos):
+    def send_x(layer, dst, slot, pos, half):
+        rows = pl.ds(pl.multiple_of(half * HALF, HALF), HALF)
         return pltpu.make_async_remote_copy(
-            src_ref=xo.at[slot, pos], dst_ref=xbuf.at[layer + 1], send_sem=xs_sem.at[slot, pos], recv_sem=xr_sem.at[layer],
+            src_ref=xo.at[slot, pos, rows], dst_ref=xbuf.at[layer + 1, rows],
+            send_sem=xs_sem.at[slot, pos, half], recv_sem=xr_sem.at[layer, half],
             device_id={"data": dst}, device_id_type=mesh_id)
 
     small = [pltpu.make_async_copy(src, dst, isem.at[k]) for k, (src, dst) in enumerate(
@@ -112,19 +114,21 @@
         slot = jnp.where((layer == 0) & (me == 1), 0, 2 * wslot + 1)
         pos = jnp.where(layer == 0, core, 0)
         wcopy(layer, 0).wait()
-
-        @pl.when((layer > 0) & jnp.logical_not(is_local(layer - 1)))
-        def _():
-            send_x(layer - 1, me, 0, 0).wait_recv()
-
-        normed = rms(xbuf[layer], ga[pl.ds(layer, 1), :])
-        qkv = jnp.dot(normed, qkvw[wslot], preferred_element_type=F32).astype(BF16).astype(F32)
-        for j in range(HEADS):
-            rows8 = pl.ds(j, ROWS, stride=8)
-            kv = j * 2 // HEADS
-            q3[rows8, :] = qkv[:, j * HD:(j + 1) * HD]
-            k3[rows8, :] = qkv[:, (HEADS + kv) * HD:(HEADS + kv + 1) * HD]
-            v3[rows8, :] = qkv[:, (HEADS + 2 + kv) * HD:(HEADS + 3 + kv) * HD]
+        fetched = (layer > 0) & jnp.logical_not(is_local(layer - 1))
+
+        def project(half):
+            @pl.when(fetched)
+            def _():
+                send_x(layer - 1, me, 0, 0, half).wait_recv()
+
+            normed = rms(xbuf[layer, pl.ds(pl.multiple_of(half * HALF, HALF), HALF)], ga[pl.ds(layer, 1), :])
+            qkv = jnp.dot(normed, qkvw[wslot], preferred_element_type=F32).astype(BF16).astype(F32)
+            for j in range(HEADS):
+                rows8 = pl.ds(half * (HALF * 8) + j, HALF, stride=8)
+                kv = j * 2 // HEADS
+                q3[rows8, :] = qkv[:, j * HD:(j + 1) * HD]
+                k3[rows8, :] = qkv[:, (HEADS + kv) * HD:(HEADS + kv + 1) * HD]
+                v3[rows8, :] = qkv[:, (HEADS + 2 + kv) * HD:(HEADS + 3 + kv) * HD]
 
         def refill(c, ok=True):
             @pl.when((c < LAYERS * CHUNKS) & ok)
@@ -172,6 +176,28 @@
             for k in range(2):
                 chunk_math(part + k)
 
+        def wait_weights(idx):
+            @pl.when(idx == core)
+            def _():
+                for k in range(3):
+                    fcopy(k).wait()
+
+            @pl.when(idx != core)
+            def _():
+                for k in range(3):
+                    fsend(k, idx).wait_recv()
+
+        def ffn(rows_h, tl, idx):
+            n2 = rms(rows_h, gf[pl.ds(tl, 1), :])
+            zrows = slice(0, rows_h.shape[0])
+            for b in range(FFN // FBLK):
+                cols = slice(b * FBLK, (b + 1) * FBLK)
+                a = jnp.dot(n2, fg[idx, :, cols], preferred_element_type=F32)
+                u = jnp.dot(n2, fu[idx, :, cols], preferred_element_type=F32)
+                zbuf[zrows, cols] = (a * jax.nn.sigmoid(a) * u).astype(BF16)
+            down = jnp.dot(zbuf[zrows, :], fd[idx], preferred_element_type=F32)
+            return (rows_h.astype(F32) + down).astype(BF16)
+
         def half_att(half, carry):
             @pl.when(half == 0)
             def _():
@@ -196,6 +222,7 @@
 
                 refill(layer * CHUNKS + 6)
 
+            project(half)
             chunk_pair(half * (CHUNKS // 2))
 
             @pl.when(half == 0)
@@ -216,6 +243,22 @@
             def _():
                 hbuf[layer, rows] = mid
                 send_h(layer, half, dst, slot, pos).start()
+
+            @pl.when(jnp.where(chip == 0, layer == 2, (layer + half == 2) & (layer > 0)))
+            def _():
+                tl = jnp.where(chip == 0, 1, 2)
+                th = jnp.where(chip == 0, half, 1 - half)
+                idx = 1 - chip
+                fslot = 2 * idx + 1
+                send_h(0, th, me, fslot, 0).wait_recv()
+
+                @pl.when((chip == 1) & (th == 0))
+                def _():
+                    wait_weights(idx)
+
+                rows = pl.ds(pl.multiple_of(th * HALF, HALF), HALF)
+                xo[fslot, 0, rows] = ffn(hin[fslot, 0, rows], tl, idx)
+                send_x(tl, peer, fslot, 0, th).start()
             return carry
 
         lax.fori_loop(0, 2, half_att, 0)
@@ -245,19 +288,15 @@
         refill(layer * CHUNKS + 7)
 
         def ffn_step(turn, carry):
-            serve0 = (layer == 2) | (turn == 1)
-            serve1 = (layer != 2) & (turn == 0)
-            serve = jnp.where(chip == 0, serve0, serve1)
-            tl = jnp.where(chip == 0, jnp.where(layer == 2, 1, layer), jnp.where(layer == 1, 2, layer))
-            todo0 = jnp.where(turn == 0, layer < 3, layer == 0) & ((layer > 0) | (me == 0))
-            todo1 = jnp.where(turn == 0, layer > 0, layer == 3)
-            todo = jnp.where(chip == 0, todo0, todo1)
-
-            @pl.when(todo)
-            def _():
-                idx = lax.rem(tl, 2)
+            serve = jnp.where(chip == 0, turn == 1, (layer == 3) & (turn == 0))
+            todo0 = jnp.where(turn == 0, layer < 2, layer == 0) & ((layer > 0) | (me == 0))
+            todo1 = jnp.where(turn == 0, layer > 1, layer == 3)
+
+            @pl.when(jnp.where(chip == 0, todo0, todo1))
+            def _():
+                idx = wslot
                 fslot = 2 * idx + jnp.where(serve, 1, 0)
-                both = tl == 0
+                both = layer == 0
 
                 @pl.when(serve)
                 def _():
@@ -269,49 +308,31 @@
                     for half in range(2):
                         send_h(0, half, me, fslot, 1).wait_recv()
 
-                first = jnp.where(serve, 1, 0) == chip
-
-                @pl.when(first & (idx == core))
-                def _():
-                    for k in range(3):
-                        fcopy(k).wait()
-
-                @pl.when(first & (idx != core))
-                def _():
-                    for k in range(3):
-                        fsend(k, idx).wait_recv()
-
-                def ffn(count):
-                    rows_h = hin[fslot, 0:count].reshape(count * ROWS, D)
-                    n2 = rms(rows_h, gf[pl.ds(tl, 1), :])
-                    zrows = slice(0, count * ROWS)
-                    for b in range(FFN // FBLK):
-                        cols = slice(b * FBLK, (b + 1) * FBLK)
-                        a = jnp.dot(n2, fg[idx, :, cols], preferred_element_type=F32)
-                        u = jnp.dot(n2, fu[idx, :, cols], preferred_element_type=F32)
-                        zbuf[zrows, cols] = (a * jax.nn.sigmoid(a) * u).astype(BF16)
-                    down = jnp.dot(zbuf[zrows, :], fd[idx], preferred_element_type=F32)
-                    xo[fslot, 0:count] = (rows_h.astype(F32) + down).astype(BF16).reshape(count, ROWS, D)
+                @pl.when(jnp.where(chip == 0, turn == 0, serve))
+                def _():
+                    wait_weights(idx)
 
                 @pl.when(both)
                 def _():
-                    ffn(2)
+                    xo[fslot] = ffn(hin[fslot].reshape(2 * ROWS, D), layer, idx).reshape(2, ROWS, D)
 
                 @pl.when(jnp.logical_not(both))
                 def _():
-                    ffn(1)
+                    xo[fslot, 0] = ffn(hin[fslot, 0], layer, idx)
 
                 @pl.when(serve)
                 def _():
-                    send_x(tl, peer, fslot, 0).start()
+                    for half in range(2):
+                        send_x(layer, peer, fslot, 0, half).start()
 
                 @pl.when(jnp.logical_not(serve))
                 def _():
-                    xbuf[tl + 1] = xo[fslot, 0]
+                    xbuf[layer + 1] = xo[fslot, 0]
 
                 @pl.when(both)
                 def _():
-                    send_x(tl, jnp.where(serve, 3, 1), fslot, 1).start()
+                    for half in range(2):
+                        send_x(layer, jnp.where(serve, 3, 1), fslot, 1, half).start()
             return carry
 
         refill(layer * CHUNKS + 8)
@@ -323,30 +344,34 @@
 
     @pl.when(chip == 0)
     def _():
-        send_x(LAYERS - 1, me, 0, 0).wait_recv()
+        for half in range(2):
+            send_x(LAYERS - 1, me, 0, 0, half).wait_recv()
 
     out[...] = xbuf[LAYERS]
 
-    for layer in range(LAYERS):
-        @pl.when(jnp.logical_not(is_local(layer)))
-        def _():
-            for half in range(2):
+    for half in range(2):
+        for layer in range(LAYERS):
+            @pl.when(jnp.logical_not(is_local(layer)))
+            def _():
                 send_h(layer, half, 0, 0, 0).wait_send()
+
+        @pl.when(me != 0)
+        def _():
+            send_x(0, me, 3, 0, half).wait_send()
+
+        @pl.when(chip == 1)
+        def _():
+            send_x(0, me, 1, 0, half).wait_send()
+
+        @pl.when(me == 0)
+        def _():
+            for slot, pos in ((0, 1), (1, 0), (1, 1), (3, 0)):
+                send_x(0, me, slot, pos, half).wait_send()
 
     @pl.when(me != 0)
     def _():
-        send_x(0, me, 3, 0).wait_send()
         for k in range(3):
             fsend(k, core).wait_send()
-
-    @pl.when(chip == 1)
-    def _():
-        send_x(0, me, 1, 0).wait_send()
-
-    @pl.when(me == 0)
-    def _():
-        for slot, pos in ((0, 1), (1, 0), (1, 1), (3, 0)):
-            send_x(0, me, slot, pos).wait_send()
 
 
 def solution(mesh):
@@ -386,7 +411,7 @@
                 pltpu.VMEM((4, 2, ROWS, D), BF16),
                 pltpu.VMEM((2 * ROWS, FFN), BF16),
                 dma((SLOTS,)), dma((SLOTS,)), dma((2, 2)), dma((3,)), dma((3,)), dma((3,)),
-                dma((LAYERS, 2)), dma((4, 2, 2)), dma((4, 2)), dma((LAYERS,)),
+                dma((LAYERS, 2)), dma((4, 2, 2)), dma((4, 2, 2)), dma((LAYERS, 2)),
                 pltpu.VMEM((LAYERS, D), F32), pltpu.VMEM((LAYERS, D), F32), pltpu.VMEM((1, ROWS), jnp.int32), dma((4,)),
             ],
             compiler_params=pltpu.CompilerParams(collective_id=0, has_side_effects=True, vmem_limit_bytes=64000000),

time: 53.8 us -> 62.5 us (1.16)
  the two profiles are of different devices: /device:TPU:0 before, /device:TPU:1 now
where the time goes in v7:
time: 62.5 us; the launch traced here: 62.4 us
  Pallas kernels  61.8 us (99%)
  local copies, waits for them, and re-layouts  0.64 us (1%)
    pallas_call x1, Pallas kernels, per_device(): pl.pallas_call(kernel, out_shape=pltpu.VMEM((ROWS, D), BF16), in_specs=[a...  61.8 us

profile of v7, /device:TPU:1, one launch (start us, length us, event | category | flops | bytes accessed | tf_op | source)
XLA Modules:
  0.0 62.4 jit_solution(5677772537941179437)
XLA Ops:
  0.0 61.8 %shard_map.109 = bf16[64,768]{1,0:T(8,128)(2,1)S(1)} custom-call(bf16[64,768]{1,0:T(8,128)(2,1)} %hid_in.1, f32[4,768]{1,0:T(4,128)} %ga_in.1, f32[4,768]{1,0:T(4,128)} %gf_in.1, s32[1,64]{1,0:T(1,128)} %bitcast.5, bf16[4,768,1280]{2,1,0:T(8,128)(2,1)} %wqkv.1, bf16[4,768,768]{2,1,0:T(8,128)(2,1)} %wout.1, bf16[4,64,512,128]{3,2,1,0:T(8,128)(2,1)} %bitcast.3, ...), custom_call_target="tpu_custom_call" | custom-call | tf_op jit(solution)/shard_map/pallas_call | solution.py:390
  61.8 0.6 %copy.13 = bf16[64,768]{1,0:T(8,128)(2,1)} copy(bf16[64,768]{1,0:T(8,128)(2,1)S(1)} %shard_map.109) | data formatting | bytes 196608

commit v8 on v7

--- a/solution.py
+++ b/solution.py
@@ -244,6 +244,33 @@
                 hbuf[layer, rows] = mid
                 send_h(layer, half, dst, slot, pos).start()
 
+            @pl.when(half == 1)
+            def _():
+                @pl.when(layer + 1 < LAYERS)
+                def _():
+                    for which in range(2):
+                        wcopy(layer + 1, which).start()
+
+                @pl.when((layer == 0) & (chip == 1))
+                def _():
+                    fsend(0, core).start()
+
+                @pl.when((layer == 0) & (me != 0))
+                def _():
+                    fsend(1, core).start()
+
+                @pl.when(jnp.where(chip == 0, (layer == 0) & (me == 1), layer == 1))
+                def _():
+                    fsend(2, core).start()
+
+                @pl.when((layer == 0) & (me == 1))
+                def _():
+                    for k in range(3):
+                        fcopy(k).start()
+
+                refill(layer * CHUNKS + 7)
+                refill(layer * CHUNKS + 8)
+
             @pl.when(jnp.where(chip == 0, layer == 2, (layer + half == 2) & (layer > 0)))
             def _():
                 tl = jnp.where(chip == 0, 1, 2)
@@ -263,30 +290,6 @@
 
         lax.fori_loop(0, 2, half_att, 0)
 
-        @pl.when(layer + 1 < LAYERS)
-        def _():
-            for which in range(2):
-                wcopy(layer + 1, which).start()
-
-        @pl.when((layer == 0) & (chip == 1))
-        def _():
-            fsend(0, core).start()
-
-        @pl.when((layer == 0) & (me != 0))
-        def _():
-            fsend(1, core).start()
-
-        @pl.when(jnp.where(chip == 0, (layer == 0) & (me == 1), layer == 1))
-        def _():
-            fsend(2, core).start()
-
-        @pl.when((layer == 0) & (me == 1))
-        def _():
-            for k in range(3):
-                fcopy(k).start()
-
-        refill(layer * CHUNKS + 7)
-
         def ffn_step(turn, carry):
             serve = jnp.where(chip == 0, turn == 1, (layer == 3) & (turn == 0))
             todo0 = jnp.where(turn == 0, layer < 2, layer == 0) & ((layer > 0) | (me == 0))
@@ -335,7 +338,6 @@
                         send_x(layer, jnp.where(serve, 3, 1), fslot, 1, half).start()
             return carry
 
-        refill(layer * CHUNKS + 8)
         lax.fori_loop(0, 2, ffn_step, 0)
         refill(layer * CHUNKS + 9)
         return carry

time: 62.5 us -> 55.8 us (0.89)
  the two profiles are of different devices: /device:TPU:1 before, /device:TPU:0 now
where the time goes in v8:
time: 55.8 us; the launch traced here: 55.7 us
  Pallas kernels  55.1 us (99%)
  local copies, waits for them, and re-layouts  0.64 us (1%)
    pallas_call x1, Pallas kernels, per_device(): pl.pallas_call(kernel, out_shape=pltpu.VMEM((ROWS, D), BF16), in_specs=[a...  55.1 us

profile of v8, /device:TPU:0, one launch (start us, length us, event | category | flops | bytes accessed | tf_op | source)
XLA Modules:
  0.0 55.7 jit_solution(2219416887317417470)
XLA Ops:
  0.0 55.1 %shard_map.109 = bf16[64,768]{1,0:T(8,128)(2,1)S(1)} custom-call(bf16[64,768]{1,0:T(8,128)(2,1)} %hid_in.1, f32[4,768]{1,0:T(4,128)} %ga_in.1, f32[4,768]{1,0:T(4,128)} %gf_in.1, s32[1,64]{1,0:T(1,128)} %bitcast.5, bf16[4,768,1280]{2,1,0:T(8,128)(2,1)} %wqkv.1, bf16[4,768,768]{2,1,0:T(8,128)(2,1)} %wout.1, bf16[4,64,512,128]{3,2,1,0:T(8,128)(2,1)} %bitcast.3, ...), custom_call_target="tpu_custom_call" | custom-call | tf_op jit(solution)/shard_map/pallas_call | solution.py:392
  55.1 0.6 %copy.13 = bf16[64,768]{1,0:T(8,128)(2,1)} copy(bf16[64,768]{1,0:T(8,128)(2,1)S(1)} %shard_map.109) | data formatting | bytes 196608

commit v9 on v6

--- a/solution.py
+++ b/solution.py
@@ -166,11 +166,23 @@
             o3[rows, :] = jnp.concatenate(outs, 0) + self_out
 
         def chunk_pair(part):
-            for k in range(2):
-                for which in range(2):
-                    kcopy(layer * CHUNKS + part + k, which).wait()
-            for k in range(2):
-                chunk_math(part + k)
+            @pl.when(layer == 0)
+            def _():
+                def one(k, carry):
+                    for which in range(2):
+                        kcopy(part + k, which).wait()
+                    chunk_math(part + k)
+                    return carry
+
+                lax.fori_loop(0, 2, one, 0)
+
+            @pl.when(layer > 0)
+            def _():
+                for k in range(2):
+                    for which in range(2):
+                        kcopy(layer * CHUNKS + part + k, which).wait()
+                for k in range(2):
+                    chunk_math(part + k)
 
         def half_att(half, carry):
             @pl.when(half == 0)

time: 53.8 us -> 53.3 us (level)
  no operation moved by 1% of the time
where the time goes in v9:
time: 53.3 us; the launch traced here: 53.2 us
  Pallas kernels  52.6 us (99%)
  local copies, waits for them, and re-layouts  0.64 us (1%)
    pallas_call x1, Pallas kernels, per_device(): pl.pallas_call(kernel, out_shape=pltpu.VMEM((ROWS, D), BF16), in_specs=[a...  52.6 us

profile of v9, /device:TPU:0, one launch (start us, length us, event | category | flops | bytes accessed | tf_op | source)
XLA Modules:
  0.0 53.2 jit_solution(18259119119926716568)
XLA Ops:
  0.0 52.6 %shard_map.109 = bf16[64,768]{1,0:T(8,128)(2,1)S(1)} custom-call(bf16[64,768]{1,0:T(8,128)(2,1)} %hid_in.1, f32[4,768]{1,0:T(4,128)} %ga_in.1, f32[4,768]{1,0:T(4,128)} %gf_in.1, s32[1,64]{1,0:T(1,128)} %bitcast.5, bf16[4,768,1280]{2,1,0:T(8,128)(2,1)} %wqkv.1, bf16[4,768,768]{2,1,0:T(8,128)(2,1)} %wout.1, bf16[4,64,512,128]{3,2,1,0:T(8,128)(2,1)} %bitcast.3, ...), custom_call_target="tpu_custom_call" | custom-call | tf_op jit(solution)/shard_map/pallas_call | solution.py:377
  52.6 0.6 %copy.13 = bf16[64,768]{1,0:T(8,128)(2,1)} copy(bf16[64,768]{1,0:T(8,128)(2,1)S(1)} %shard_map.109) | data formatting | bytes 196608

commit v10 on v9

--- a/solution.py
+++ b/solution.py
@@ -200,13 +200,7 @@
 
             @pl.when(half == 1)
             def _():
-                @pl.when(layer == 0)
-                def _():
-                    for c in (4, 5):
-                        for which in range(2):
-                            kcopy(c, which).start()
-
-                refill(layer * CHUNKS + 6)
+                refill(jnp.where(layer == 0, CHUNKS, layer * CHUNKS + 6))
 
             chunk_pair(half * (CHUNKS // 2))
 
@@ -232,11 +226,14 @@
 
         lax.fori_loop(0, 2, half_att, 0)
 
-        @pl.when(layer + 1 < LAYERS)
-        def _():
+        def next_weights():
             for which in range(2):
                 wcopy(layer + 1, which).start()
 
+        @pl.when((layer + 1 < LAYERS) & ((layer != 2) | (chip == 1)))
+        def _():
+            next_weights()
+
         @pl.when((layer == 0) & (chip == 1))
         def _():
             fsend(0, core).start()
@@ -254,7 +251,13 @@
             for k in range(3):
                 fcopy(k).start()
 
-        refill(layer * CHUNKS + 7)
+        refill(CHUNKS + 1, layer == 0)
+
+        @pl.when(chip == 1)
+        def _():
+            refill(CHUNKS + 2, layer == 0)
+            refill(layer * CHUNKS + 7)
+            refill(layer * CHUNKS + 8)
 
         def ffn_step(turn, carry):
             serve0 = (layer == 2) | (turn == 1)
@@ -324,9 +327,21 @@
                 @pl.when(both)
                 def _():
                     send_x(tl, jnp.where(serve, 3, 1), fslot, 1).start()
+
+            @pl.when(chip == 0)
+            def _():
+                @pl.when((layer == 2) & (turn == 0))
+                def _():
+                    next_weights()
+
+                @pl.when((layer == 0) & (turn == 1))
+                def _():
+                    for which in range(2):
+                        kcopy(CHUNKS + 3, which).start()
+
+                refill(jnp.where((layer == 0) & (turn == 0), CHUNKS + 2, layer * CHUNKS + 7 + turn))
             return carry
 
-        refill(layer * CHUNKS + 8)
         lax.fori_loop(0, 2, ffn_step, 0)
         refill(layer * CHUNKS + 9)
         return carry

time: 53.3 us -> 53.4 us (level)
  no operation moved by 1% of the time
where the time goes in v10:
time: 53.4 us; the launch traced here: 53.3 us
  Pallas kernels  52.6 us (99%)
  local copies, waits for them, and re-layouts  0.64 us (1%)
    pallas_call x1, Pallas kernels, per_device(): pl.pallas_call(kernel, out_shape=pltpu.VMEM((ROWS, D), BF16), in_specs=[a...  52.6 us

profile of v10, /device:TPU:0, one launch (start us, length us, event | category | flops | bytes accessed | tf_op | source)
XLA Modules:
  0.0 53.3 jit_solution(7736908634173078208)
XLA Ops:
  0.0 52.6 %shard_map.109 = bf16[64,768]{1,0:T(8,128)(2,1)S(1)} custom-call(bf16[64,768]{1,0:T(8,128)(2,1)} %hid_in.1, f32[4,768]{1,0:T(4,128)} %ga_in.1, f32[4,768]{1,0:T(4,128)} %gf_in.1, s32[1,64]{1,0:T(1,128)} %bitcast.5, bf16[4,768,1280]{2,1,0:T(8,128)(2,1)} %wqkv.1, bf16[4,768,768]{2,1,0:T(8,128)(2,1)} %wout.1, bf16[4,64,512,128]{3,2,1,0:T(8,128)(2,1)} %bitcast.3, ...), custom_call_target="tpu_custom_call" | custom-call | tf_op jit(solution)/shard_map/pallas_call | solution.py:392
  52.6 0.6 %copy.13 = bf16[64,768]{1,0:T(8,128)(2,1)} copy(bf16[64,768]{1,0:T(8,128)(2,1)S(1)} %shard_map.109) | data formatting | bytes 196608

commit v11 on v9

--- a/solution.py
+++ b/solution.py
@@ -184,6 +184,11 @@
                 for k in range(2):
                     chunk_math(part + k)
 
+        def mid_rows(base, rows, count):
+            attn = jnp.concatenate([o3[pl.ds(base + j, count, stride=8), :] for j in range(HEADS)], 1).astype(BF16)
+            proj = jnp.dot(attn, outw[wslot], preferred_element_type=F32)
+            return (xbuf[layer, rows].astype(F32) + proj).astype(BF16)
+
         def half_att(half, carry):
             @pl.when(half == 0)
             def _():
@@ -214,23 +219,18 @@
             def _():
                 wcopy(layer, 1).wait()
 
-            base = half * (HALF * 8)
-            attn = jnp.concatenate([o3[pl.ds(base + j, HALF, stride=8), :] for j in range(HEADS)], 1).astype(BF16)
-            proj = jnp.dot(attn, outw[wslot], preferred_element_type=F32)
-            rows = pl.ds(pl.multiple_of(half * HALF, HALF), HALF)
-            mid = (xbuf[layer, rows].astype(F32) + proj).astype(BF16)
-
-            @pl.when(local)
-            def _():
-                hin[2 * wslot, 0, rows] = mid
-
             @pl.when(jnp.logical_not(local))
             def _():
-                hbuf[layer, rows] = mid
+                rows = pl.ds(pl.multiple_of(half * HALF, HALF), HALF)
+                hbuf[layer, rows] = mid_rows(half * (HALF * 8), rows, HALF)
                 send_h(layer, half, dst, slot, pos).start()
             return carry
 
         lax.fori_loop(0, 2, half_att, 0)
+
+        @pl.when(local)
+        def _():
+            hin[2 * wslot, 0] = mid_rows(0, pl.ds(0, ROWS), ROWS)
 
         @pl.when(layer + 1 < LAYERS)
         def _():

time: 53.3 us -> 52.7 us (0.989)
  Pallas kernels: 52.6 us -> 51.9 us
    pallas_call x1, Pallas kernels: 52.6 us -> 51.9 us  [per_device(): pl.pallas_call(kernel, out_shape=pltpu.VMEM((ROWS, D), BF16), in_specs=[a...]
where the time goes in v11:
time: 52.7 us; the launch traced here: 52.5 us
  Pallas kernels  51.9 us (98%)
  local copies, waits for them, and re-layouts  0.64 us (1%)
    pallas_call x1, Pallas kernels, per_device(): pl.pallas_call(kernel, out_shape=pltpu.VMEM((ROWS, D), BF16), in_specs=[a...  51.9 us

profile of v11, /device:TPU:0, one launch (start us, length us, event | category | flops | bytes accessed | tf_op | source)
XLA Modules:
  0.0 52.5 jit_solution(9706982513726434816)
XLA Ops:
  0.0 51.9 %shard_map.109 = bf16[64,768]{1,0:T(8,128)(2,1)S(1)} custom-call(bf16[64,768]{1,0:T(8,128)(2,1)} %hid_in.1, f32[4,768]{1,0:T(4,128)} %ga_in.1, f32[4,768]{1,0:T(4,128)} %gf_in.1, s32[1,64]{1,0:T(1,128)} %bitcast.5, bf16[4,768,1280]{2,1,0:T(8,128)(2,1)} %wqkv.1, bf16[4,768,768]{2,1,0:T(8,128)(2,1)} %wout.1, bf16[4,64,512,128]{3,2,1,0:T(8,128)(2,1)} %bitcast.3, ...), custom_call_target="tpu_custom_call" | custom-call | tf_op jit(solution)/shard_map/pallas_call | solution.py:377
  51.9 0.6 %copy.13 = bf16[64,768]{1,0:T(8,128)(2,1)} copy(bf16[64,768]{1,0:T(8,128)(2,1)S(1)} %shard_map.109) | data formatting | bytes 196608

commit v12 on v11

--- a/solution.py
+++ b/solution.py
@@ -36,7 +36,7 @@
            ksem, vsem, wsem, fsem, fs_sem, fr_sem, hs_sem, hr_sem, xs_sem, xr_sem, ga, gf, lens, isem):
     me = lax.axis_index("data")
     chip, core = lax.shift_right_logical(me, 1), lax.rem(me, 2)
-    mate, peer = chip * 2 + (1 - core), lax.rem(me + 2, 4)
+    mate, peer = chip * 2 + (1 - core), 3 - me
     mesh_id = pl.DeviceIdType.MESH
 
     def kcopy(c, which):
@@ -315,7 +315,7 @@
 
                 @pl.when(serve)
                 def _():
-                    send_x(tl, peer, fslot, 0).start()
+                    send_x(tl, jnp.where(both, 2, peer), fslot, 0).start()
 
                 @pl.when(jnp.logical_not(serve))
                 def _():

time: 52.7 us -> 52.7 us (level)
  no operation moved by 1% of the time
where the time goes in v12:
time: 52.7 us; the launch traced here: 52.6 us
  Pallas kernels  52 us (99%)
  local copies, waits for them, and re-layouts  0.64 us (1%)
    pallas_call x1, Pallas kernels, per_device(): pl.pallas_call(kernel, out_shape=pltpu.VMEM((ROWS, D), BF16), in_specs=[a...  52 us

profile of v12, /device:TPU:0, one launch (start us, length us, event | category | flops | bytes accessed | tf_op | source)
XLA Modules:
  0.0 52.6 jit_solution(11501231464102211979)
XLA Ops:
  0.0 52.0 %shard_map.109 = bf16[64,768]{1,0:T(8,128)(2,1)S(1)} custom-call(bf16[64,768]{1,0:T(8,128)(2,1)} %hid_in.1, f32[4,768]{1,0:T(4,128)} %ga_in.1, f32[4,768]{1,0:T(4,128)} %gf_in.1, s32[1,64]{1,0:T(1,128)} %bitcast.5, bf16[4,768,1280]{2,1,0:T(8,128)(2,1)} %wqkv.1, bf16[4,768,768]{2,1,0:T(8,128)(2,1)} %wout.1, bf16[4,64,512,128]{3,2,1,0:T(8,128)(2,1)} %bitcast.3, ...), custom_call_target="tpu_custom_call" | custom-call | tf_op jit(solution)/shard_map/pallas_call | solution.py:377
  52.0 0.6 %copy.13 = bf16[64,768]{1,0:T(8,128)(2,1)} copy(bf16[64,768]{1,0:T(8,128)(2,1)S(1)} %shard_map.109) | data formatting | bytes 196608
